TPU v7x, 32 devices: a whole 2x2x4 slice. The times are simulated.
32 devices in a mesh: ctx: 8 (over z, y), fsdp: 4 (over x, core).
Axes of the slice: x: 2, y: 2, z: 4, core: 2. Of those that a mesh axis runs over, the one named last changes fastest.
Arguments:
- hidden: bfloat16 [4, 1024, 1536], P('fsdp', 'ctx'), may hold values from -6 to 6
- routes: int32 [4, 1024, 8], P('fsdp', 'ctx'), may hold values from 0 to 31, all different within a row; in each aligned block of 128 rows (0 to 127, 128 to 255, ..., all dimensions but the last counted through in order) at most 40 rows name the same one
- attn_norm: bfloat16 [1536], P(('ctx', 'fsdp')), may hold values from 0.5 to 1.5
- ffn_norm: bfloat16 [1536], P(('ctx', 'fsdp')), may hold values from 0.5 to 1.5
- w_q: bfloat16 [1536, 1536], P(('ctx', 'fsdp')), may hold values from -0.625 to 0.625
- key_weight: bfloat16 [1536, 512], P(('ctx', 'fsdp')), may hold values from -0.625 to 0.625
- value_weight: bfloat16 [1536, 512], P(('ctx', 'fsdp')), may hold values from -0.15625 to 0.15625
- w_o: bfloat16 [1536, 1536], P(('ctx', 'fsdp')), may hold values from -1.75 to 1.75
- router: bfloat16 [1536, 32], P(('ctx', 'fsdp')), may hold values from -0.3125 to 0.3125
- expert_in: bfloat16 [32, 1536, 1024], P('ctx', 'fsdp'), may hold values from -0.15625 to 0.15625
- expert_out: bfloat16 [32, 1536, 512], P('ctx', 'fsdp'), may hold values from -0.25 to 0.25
- cotangent: float32 [4, 1024, 1536], P('fsdp', 'ctx'), may hold values from -6 to 6
Outputs:
- layer_out: bfloat16 [4, 1024, 1536], P('fsdp', 'ctx')
- grad_hidden: float32 [4, 1024, 1536], P('fsdp', 'ctx')
- grad_attn_norm: float32 [1536], P(('ctx', 'fsdp'))
- grad_ffn_norm: float32 [1536], P(('ctx', 'fsdp'))
- grad_w_q: float32 [1536, 1536], P(('ctx', 'fsdp'))
- grad_w_k: float32 [1536, 512], P(('ctx', 'fsdp'))
- grad_w_v: float32 [1536, 512], P(('ctx', 'fsdp'))
- grad_w_o: float32 [1536, 1536], P(('ctx', 'fsdp'))
- grad_router: float32 [1536, 32], P(('ctx', 'fsdp'))
- grad_expert_in: float32 [32, 1536, 1024], P('ctx', 'fsdp')
- grad_expert_out: float32 [32, 1536, 512], P('ctx', 'fsdp')
Inputs may be any that keep to these rules, and one draw needn't show every extreme that they name: `routes`: in the tokens of one block of 128, no expert is named more than 40 times, a bound that some block reaches.
All inputs are finite; a program needn't handle non-finite values.
Results may differ from a plain program's by a relative error of at most 0.033.
Values may be sent and summed in bfloat16 or wider, within the bound.
A program may use at most 256 MiB of HBM per device.

v0:
```python
import functools
import itertools

import jax
import jax.numpy as jnp
from jax import lax
from jax.experimental import pallas as pl
from jax.experimental.pallas import tpu as pltpu
from jax.sharding import PartitionSpec as P


NY = 2
NZ = 4
NX = 2
NC = 2
DEV = pl.DeviceIdType.MESH
CTX, FSDP = "ctx", "fsdp"
Z, Y, X, C = 0, 1, 2, 3
SIZES = {Z: NZ, Y: NY, X: NX, C: NC}
UP, DOWN = 4, 5


class Plan:
    def __init__(self, ref, order, index, rows=None, view=None):
        self.ref, self.order, self.index, self.rows, self.view = ref, order, index, rows, view
        self.blocks = 1
        for d in index:
            self.blocks *= SIZES[d]


class Place:
    def __init__(self):
        ctx = lax.axis_index(CTX)
        fsdp = lax.axis_index(FSDP)
        self.at = {Z: ctx // NY, Y: ctx % NY, X: fsdp // NC, C: fsdp % NC}
        z = self.at[Z]
        low = z < NZ // 2
        base = jnp.where(low, z, NZ - 1 - z)
        near = [base, 1 - base, jnp.int32(2), jnp.int32(3)]
        self.order = [z] + [jnp.where(low, k, NZ - 1 - k) for k in near[1:]]

    def device(self, dim, value):
        spot = dict(self.at)
        spot[dim] = value
        return (spot[Z] * NY + spot[Y], spot[X] * NC + spot[C])

    def across(self, dim):
        return self.device(dim, 1 - self.at[dim])

    def along(self, step):
        return self.device(Z, self.at[Z] + step)

    def coords(self, z_from, flips):
        spot = {d: (1 - self.at[d] if d in flips else self.at[d]) for d in (Y, X, C)}
        spot[Z] = z_from
        return spot


def flat_index(spot, dims):
    index = 0
    for d in dims:
        index = index * SIZES[d] + spot[d]
    return index


def subsets(dims):
    return [c for n in range(len(dims) + 1) for c in itertools.combinations(dims, n)]


def hail(place, dims, more=()):
    barrier = pltpu.get_barrier_semaphore()
    z = place.at[Z]
    count = jnp.int32(0)
    for d in dims:
        if d == Z:
            @pl.when(z > 0)
            def _():
                pl.semaphore_signal(barrier, inc=1, device_id=place.along(-1), device_id_type=DEV)

            @pl.when(z < NZ - 1)
            def _():
                pl.semaphore_signal(barrier, inc=1, device_id=place.along(1), device_id_type=DEV)

            count = count + jnp.where(z > 0, 1, 0) + jnp.where(z < NZ - 1, 1, 0)
        else:
            pl.semaphore_signal(barrier, inc=1, device_id=place.across(d), device_id_type=DEV)
            count = count + 1
    for device in more:
        pl.semaphore_signal(barrier, inc=1, device_id=device, device_id_type=DEV)
        count = count + 1
    return count


def meet(count):
    pl.semaphore_wait(pltpu.get_barrier_semaphore(), count)


def gather_events(order):
    pairs = [d for d in order if d != Z]
    events = [(k, f) for k in range(NZ) for f in subsets(pairs)]
    return sorted(events, key=lambda e: (e[0] + len(e[1]), len(e[1])))


def gather_sends(order, k, flips):
    z_at = order.index(Z)
    last = max([order.index(d) for d in flips] + ([z_at] if k > 0 else []) + [-1])
    out = []
    for position, d in enumerate(order):
        if position > last:
            out.extend([UP, DOWN] if d == Z else [d])
    if k > 0 and last == z_at:
        out.extend([UP, DOWN])
    return out


def gather_kernel(plans, *refs):
    w_q, w_k, w_v, w_o, router, first_gain, second_gain, first_w, second_w = refs[:9]
    outs, (mine, *others) = refs[9:11], refs[11:14]
    send_sem, recv_sem, own_sem, stage, load_sem, store_sem, pack_one, pack_two = refs[14:]
    ins = pack_one, pack_two
    place = Place()
    count_here = hail(place, (Z, Y, X, C))
    held = mine.shape[0]
    split = first_w.shape[2]
    loads = []
    for side in range(2):
        base = (place.at[C] if side == 0 else 1 - place.at[C]) * held
        for e in range(held):
            to = stage.at[side * held + e]
            for w, at in ((first_w, pl.ds(0, split)), (second_w, pl.ds(split, second_w.shape[2]))):
                loads.append(pltpu.make_async_copy(w.at[base + e], to.at[:, at], load_sem.at[len(loads)]))
    for copy in loads:
        copy.start()
    stores = [pltpu.make_async_copy(stage.at[pl.ds(0, held)], mine, store_sem.at[0])] + [
        pltpu.make_async_copy(stage.at[pl.ds(held + e, 1)], out, store_sem.at[1 + e]) for e, out in enumerate(others)
    ]
    at = 0
    for w in (w_q, w_k, w_v):
        pack_one[:, at : at + w.shape[1]] = w[...]
        at += w.shape[1]
    model = w_o.shape[1]
    rows = w_o.shape[0]
    pack_two[:, :model] = w_o[...]
    same = lax.broadcasted_iota(jnp.int32, (rows, rows), 0) == lax.broadcasted_iota(jnp.int32, (rows, rows), 1)
    upright = lambda gain: jnp.sum(jnp.where(same, gain[...].astype(jnp.float32), 0.0), axis=1, keepdims=True)
    lane = lax.broadcasted_iota(jnp.int32, (1, 128), 1)
    count = router.shape[0]
    small = jnp.where(lane == count, upright(first_gain), jnp.where(lane == count + 1, upright(second_gain), 0.0))
    pack_two[:, model:] = small.astype(pack_two.dtype)
    pack_two[:, model : model + count] = lax.dot_general(
        same.astype(jnp.float32).astype(router.dtype), router[...], (((1,), (1,)), ((), ())),
        preferred_element_type=jnp.float32,
    ).astype(pack_two.dtype)
    z = place.at[Z]
    meet(count_here)
    pending = []
    slot = 0
    queue = []
    for n, plan in enumerate(plans):
        for rank, event in enumerate(gather_events(plan.order)):
            queue.append((rank / len(gather_events(plan.order)), n, event))
    queue.sort(key=lambda q: (q[0], q[1]))
    bases = [sum(p.blocks for p in plans[:n]) for n in range(len(plans))]
    for turn_at, (_, n, (k, flips)) in enumerate(queue):
        if turn_at == len(queue) // 3:
            for copy in loads:
                copy.wait()
            for copy in stores:
                copy.start()
        plan = plans[n]
        src = ins[plan.ref]
        out = outs[plan.ref]
        rows = plan.rows
        z_from = place.order[k]
        spot = place.coords(z_from, flips)
        index = flat_index(spot, plan.index)
        own = k == 0 and not flips
        if plan.view is not None:
            target = plan.view(out, spot, rows)
            source = src.at[:, pl.ds(rows[0], rows[1])] if own else target
        else:
            target = out.at[index] if rows is None else out.at[index, pl.ds(rows[0], rows[1])]
            source = (src if rows is None else src.at[pl.ds(rows[0], rows[1])]) if own else target
        sem = recv_sem.at[bases[n] + index]
        if not own:
            pltpu.make_async_remote_copy(
                src_ref=target, dst_ref=target, send_sem=own_sem.at[0], recv_sem=sem,
                device_id=place.across(C), device_id_type=DEV,
            ).wait_recv()
        for way in gather_sends(plan.order, k, flips):
            if way in (UP, DOWN):
                step = 1 if way == UP else -1
                go = z < NZ - 1 if way == UP else z > 0
                if k > 0:
                    go = jnp.logical_and(go, z_from < z if way == UP else z_from > z)
                dest = place.device(Z, jnp.clip(z + step, 0, NZ - 1))
            else:
                go, dest = None, place.across(way)
            copy = pltpu.make_async_remote_copy(
                src_ref=source, dst_ref=target, send_sem=send_sem.at[slot], recv_sem=sem,
                device_id=dest, device_id_type=DEV,
            )
            slot += 1
            if go is None:
                copy.start()
            else:
                pl.when(go)(copy.start)
            pending.append((go, copy.wait_send))
        if own:
            copy = pltpu.make_async_copy(source, target, own_sem.at[1 + n])
            copy.start()
            pending.append((None, copy.wait))
    for copy in stores:
        copy.wait()
    for go, wait in pending:
        if go is None:
            wait()
        else:
            pl.when(go)(wait)


def gather_weights(weights, experts, plans, collective_id):
    sends = sum(len(gather_sends(p.order, k, f)) for p in plans for k, f in gather_events(p.order))
    rows = weights[0].shape[0]
    bf = weights[0].dtype
    widths = [sum(w.shape[1] for w in weights[:3]), weights[3].shape[1] + 128]
    held = experts[0].shape[0] // NC
    pack = (experts[0].shape[1], experts[0].shape[2] + experts[1].shape[2])
    apart = pl.BlockSpec(memory_space=pl.ANY)
    dma = pltpu.SemaphoreType.DMA
    return pl.pallas_call(
        functools.partial(gather_kernel, plans),
        out_shape=[jax.ShapeDtypeStruct((plans[0].blocks, rows, w), bf) for w in widths]
        + [jax.ShapeDtypeStruct((n,) + pack, bf) for n in [held] + [1] * held],
        in_specs=[pl.BlockSpec(memory_space=pltpu.VMEM)] * len(weights) + [apart] * 2,
        out_specs=[apart] * (3 + held),
        scratch_shapes=[
            dma((sends,)),
            dma((sum(p.blocks for p in plans),)),
            dma((1 + len(plans),)),
            pltpu.VMEM((NC * held,) + pack, bf),
            dma((2 * NC * held,)),
            dma((1 + held,)),
        ]
        + [pltpu.VMEM((rows, w), bf) for w in widths],
        compiler_params=pltpu.CompilerParams(collective_id=collective_id, has_side_effects=True),
        name="gather_weights",
    )(*weights, *experts)


def add_into(acc, other):
    acc[...] = (acc[...].astype(jnp.float32) + other[...].astype(jnp.float32)).astype(acc.dtype)


class Gather:
    def __init__(self, place, plan, src, out, send_sem, recv_sem, spare_sem, slot, base):
        self.place, self.plan, self.src, self.out = place, plan, src, out
        self.send_sem, self.recv_sem, self.spare_sem = send_sem, recv_sem, spare_sem
        self.slot, self.base = slot, base
        self.pending = []

    @staticmethod
    def sends(plan):
        return sum(len(gather_sends(plan.order, k, f)) for k, f in gather_events(plan.order))

    def goes(self, way, k):
        z, z_from = self.place.at[Z], self.place.order[k]
        if way == UP:
            return z < NZ - 1 if k == 0 else jnp.logical_and(z < NZ - 1, z_from < z)
        return z > 0 if k == 0 else jnp.logical_and(z > 0, z_from > z)

    def part(self, ref):
        rows = self.plan.rows
        return ref if rows is None else ref.at[pl.ds(rows[0], rows[1])]

    def step(self, k, flips):
        place, plan = self.place, self.plan
        index = flat_index(place.coords(place.order[k], flips), plan.index)
        target = self.part(self.out.at[index])
        sem = self.recv_sem.at[self.base + index]
        source = target
        if k == 0 and not flips:
            source = self.part(self.src)
        else:
            pltpu.make_async_remote_copy(
                src_ref=target, dst_ref=target, send_sem=self.spare_sem, recv_sem=sem,
                device_id=place.across(C), device_id_type=DEV,
            ).wait_recv()
        for way in gather_sends(plan.order, k, flips):
            if way in (UP, DOWN):
                dest = place.device(Z, jnp.clip(place.at[Z] + (1 if way == UP else -1), 0, NZ - 1))
            else:
                dest = place.across(way)
            copy = pltpu.make_async_remote_copy(
                src_ref=source, dst_ref=target, send_sem=self.send_sem.at[self.slot], recv_sem=sem,
                device_id=dest, device_id_type=DEV,
            )
            if way in (UP, DOWN):
                pl.when(self.goes(way, k))(copy.start)
            else:
                copy.start()
            self.pending.append((way, k, self.slot))
            self.slot += 1

    def finish(self):
        for way, k, slot in self.pending:
            block = self.part(self.src)
            copy = pltpu.make_async_remote_copy(
                src_ref=block, dst_ref=block, send_sem=self.send_sem.at[slot], recv_sem=self.spare_sem,
                device_id=self.place.across(C), device_id_type=DEV,
            )
            if way in (UP, DOWN):
                pl.when(self.goes(way, k))(copy.wait_send)
            else:
                copy.wait_send()


class Reduce:
    def __init__(self, place, plan, held, levels, chain, send_sem, recv_sem, spare_sem):
        self.place, self.plan, self.held, self.levels, self.chain = place, plan, held, levels, chain
        self.send_sem, self.recv_sem, self.spare_sem = send_sem, recv_sem, spare_sem
        self.order, self.chain_at, self.kept, counts = Reduce.shape(plan)
        self.base = [sum(counts[:p]) for p in range(len(counts))]
        self.slot = 0

    @staticmethod
    def shape(plan):
        order = plan.order if Z in plan.order else plan.order + (Z,)
        at = order.index(Z)
        kept = [subsets(tuple(d for d in order[p + 1 :] if d != Z)) for p in range(len(order))]
        times = [NZ if p < at else NZ + 1 if p == at else 1 for p in range(len(order))]
        return order, at, kept, [n * len(f) for n, f in zip(times, kept)]

    @staticmethod
    def counts(plan):
        _, at, kept, counts = Reduce.shape(plan)
        buffers = counts[:at] + counts[at + 1 :] + [counts[at]]
        return buffers, sum(counts) - 2 * len(kept[at]), sum(counts)

    def level_of(self, p):
        return self.levels[p if p < self.chain_at else p - 1]

    def push(self, source, target, sem, dest):
        copy = pltpu.make_async_remote_copy(
            src_ref=source, dst_ref=target, send_sem=self.send_sem.at[self.slot], recv_sem=sem,
            device_id=dest, device_id_type=DEV,
        )
        self.slot += 1
        copy.start()

    def arrived(self, target, sem):
        pltpu.make_async_remote_copy(
            src_ref=target, dst_ref=target, send_sem=self.spare_sem, recv_sem=sem,
            device_id=self.place.across(C), device_id_type=DEV,
        ).wait_recv()

    def block(self, k, flips):
        return self.held.at[flat_index(self.place.coords(self.place.order[k], flips), self.plan.index)]

    def spot(self, p, k, flips):
        at = self.kept[p].index(flips)
        return at if p > self.chain_at else self.place.order[k] * len(self.kept[p]) + at

    def send(self, p, k, flips):
        dim = self.order[p]
        spot = self.spot(p, k, tuple(d for d in flips if d != dim))
        self.push(
            self.block(k, flips), self.level_of(p).at[spot],
            self.recv_sem.at[self.base[p] + spot], self.place.across(dim),
        )

    def first(self, k):
        for f in self.kept[0]:
            self.send(0, k, (self.order[0],) + f)

    def forward(self, p, k, flips):
        later = p + 1
        if later < len(self.order) and self.order[later] in flips:
            self.send(later, k, flips)

    def level(self, p, k):
        for f in sorted(self.kept[p], key=lambda f: -len(f)):
            spot = self.spot(p, k, f)
            self.arrived(self.level_of(p).at[spot], self.recv_sem.at[self.base[p] + spot])
            add_into(self.block(k, f), self.level_of(p).at[spot])
            self.forward(p, k, f)

    def link(self, spot, n):
        at = spot * len(self.kept[self.chain_at]) + n
        return self.chain.at[at], self.recv_sem.at[self.base[self.chain_at] + at]

    def along(self, k):
        z = self.place.at[Z]
        dest = self.place.order[k]
        up = dest > z
        for n, f in enumerate(self.kept[self.chain_at]):
            mine = self.block(k, f)
            target, sem = self.link(dest + jnp.where(up, 1, 0), n)

            @pl.when(jnp.where(up, z > 0, z < NZ - 1))
            def _():
                self.arrived(target, sem)
                add_into(mine, target)

            self.push(mine, target, sem, self.place.along(jnp.where(up, 1, -1)))

    def settle(self):
        z = self.place.at[Z]
        kept = self.kept[self.chain_at]
        for f in sorted(kept, key=lambda f: -len(f)):
            mine = self.block(0, f)
            for go, spot in ((z > 0, z + 1), (z < NZ - 1, z)):
                target, sem = self.link(spot, kept.index(f))

                @pl.when(go)
                def _():
                    self.arrived(target, sem)
                    add_into(mine, target)

            self.forward(self.chain_at, 0, f)

    def last(self, out, base=None):
        if self.chain_at == len(self.order) - 1:
            self.settle()
        total = self.block(0, ())[...].astype(jnp.float32)
        if base is not None:
            total = base[...] + total
        out[...] = total.astype(out.dtype)

    def at_time(self, t):
        far = list(reversed(range(NZ)))
        at = self.chain_at
        out = [functools.partial(self.level, p, far[t - p]) for p in range(at) if 0 <= t - p < NZ]
        if 0 <= t - at < NZ - 1:
            out.append(functools.partial(self.along, far[t - at]))
        if t - at == NZ - 1 and at < len(self.order) - 1:
            out.append(self.settle)
        out += [functools.partial(self.level, p, 0) for p in range(at + 1, len(self.order)) if t == NZ - 1 + p]
        return out

    def steps(self):
        return [step for t in range(NZ + len(self.order)) for step in self.at_time(t)]

    def finish(self):
        block = self.level_of(0).at[0]
        for slot in range(self.slot):
            pltpu.make_async_remote_copy(
                src_ref=block, dst_ref=block, send_sem=self.send_sem.at[slot], recv_sem=self.spare_sem,
                device_id=self.place.across(C), device_id_type=DEV,
            ).wait_send()


def tile_up(n, m):
    return (n + m - 1) // m * m


def columns_of(width, chunk=512):
    return [(i, min(chunk, width - i)) for i in range(0, width, chunk)]


def moe_kernel(plans, back, width, hidden, cap, *refs):
    payload, cots, w_own, w_x, w_core, w_core_last, w_both, w_send = refs[:8]
    gin_out, part_out = refs[8:10]
    grads = refs[10:14]
    (
        seen, cot_seen, weights, taken, cot_taken, rows_buf, scaled, grad_act, pick, stage,
        lvl_b0, lvl_b1, chain_b, lvl_c0, lvl_c1, chain_c,
        send_sem, recv_sem, spare_sem, send_b, recv_b, send_c, recv_c, load_sem, store_sem, part_sem, piece_sem,
    ) = refs[14:]
    bf, f32 = jnp.bfloat16, jnp.float32
    place = Place()
    count = payload.shape[0]
    pair = 2 * cap
    wide = width + 128
    quarter = width // (NX * NC)
    half = NZ * pair
    lanes = pick.shape[2]
    held = weights.shape[0]
    fsdp = place.at[X] * NC + place.at[C]
    first = (((place.at[Z] * NY + place.at[Y]) * NC) + place.at[C]) * held

    there = (place.at[Z] * NY + place.at[Y], (1 - place.at[X]) * NC + 1 - place.at[C])
    count_here = hail(place, (Z, Y, C), (there,))
    loads = []
    rows_of = lambda owner: pl.ds(pl.multiple_of(owner * quarter, quarter), quarter)
    sources = [(w_own, e, e, 0) for e in range(held)] + [(w_x, e, e, 2) for e in range(held)]
    sources += [(w_core, 0, 0, 1), (w_core_last, 0, held - 1, 1), (w_both, 0, 0, 3)]
    for ref, at, e, j in sources:
        loads.append(pltpu.make_async_copy(ref.at[at], weights.at[e, rows_of(fsdp ^ j)], load_sem.at[len(loads)]))
    piece = pltpu.make_async_remote_copy(
        src_ref=w_send.at[0], dst_ref=weights.at[held - 1, rows_of(fsdp)],
        send_sem=piece_sem.at[0], recv_sem=piece_sem.at[1], device_id=there, device_id_type=DEV,
    )
    base_of = lambda h, k: (jnp.where(h == 0, place.at[C], 1 - place.at[C]) * NZ + place.order[k]) * NY
    cot_loads = {}
    for k in range(NZ):
        for h in range(2):
            at = pl.ds(base_of(h, k), NY)
            cot_loads[(h, k)] = pltpu.make_async_copy(cots.at[at], cot_seen.at[at], load_sem.at[len(loads) + len(cot_loads)])

    meet(count_here)
    piece.start()
    ways = []
    send_at = 0
    for n, plan in enumerate(plans):
        ways.append(Gather(place, plan, payload, seen, send_sem, recv_sem, spare_sem, send_at, n * plan.blocks))
        send_at += Gather.sends(plan)
    for way in ways:
        way.step(0, ())
    for key in cot_loads:
        cot_loads[key].start()
    for copy in loads:
        copy.start()
    seen[flat_index(place.at, plans[0].index)] = payload[...]

    row_id = lax.broadcasted_iota(jnp.int32, (NY * count, NY * count), 0)
    col_id = lax.broadcasted_iota(jnp.int32, (NY * count, NY * count), 1)
    earlier = jnp.logical_and(col_id < row_id, col_id // count == row_id // count).astype(bf)
    lane_id = lax.broadcasted_iota(jnp.int32, (1, 128), 1)
    here = [(lane_id == first + e).astype(f32) for e in range(held)]
    pick_lane = lax.broadcasted_iota(jnp.int32, (NY * count, lanes), 1).astype(f32)
    y_shift = (lax.broadcasted_iota(jnp.int32, (NY * count, 1), 0) // count * cap).astype(f32)

    row_of = lambda h, k: (k * NC + h) * pair

    def dispatch(source, target, h, k, cols):
        at = pl.ds(base_of(h, k), NY)
        r = row_of(h, k)
        for c0, cn in cols:
            block = source[at, :, c0 : c0 + cn].reshape(NY * count, cn)
            got = lax.dot_general(
                pick[h * NZ + k], block, (((0,), (0,)), ((), ())), preferred_element_type=f32
            ).astype(bf)
            for e in range(held):
                target[e, r : r + pair, c0 : c0 + cn] = got[e * pair : (e + 1) * pair]

    def cot_chunk(h, k):
        cot_loads[(h, k)].wait()
        at = pl.ds(base_of(h, k), NY)
        chosen = cot_seen[at, :, width:wide].reshape(NY * count, 128)
        before = jnp.dot(earlier, chosen, preferred_element_type=f32)
        picked = None
        for e in range(held):
            is_here = jnp.sum(chosen.astype(f32) * here[e], axis=1, keepdims=True)
            slot = jnp.sum(before * here[e], axis=1, keepdims=True) + y_shift + e * pair
            target = jnp.where(is_here > 0.5, slot, -1.0)
            hit = pick_lane == target
            picked = hit if picked is None else jnp.logical_or(picked, hit)
        pick[h * NZ + k] = picked.astype(f32).astype(bf)
        dispatch(cot_seen, cot_taken, h, k, columns_of(width))

    def hidden_chunk(h, e, n, tile):
        rows = pl.ds(h * half, half)
        tokens_in = taken[e, rows, :width]
        gate = jnp.sum(taken[e, rows, width:wide].astype(f32) * here[e], axis=1, keepdims=True)
        col = n * tile
        g = jnp.dot(tokens_in, weights[e, :, col : col + tile], preferred_element_type=f32)
        u = jnp.dot(tokens_in, weights[e, :, hidden + col : hidden + col + tile], preferred_element_type=f32)
        raw = jnp.dot(
            cot_taken[e, rows, :], weights[e, :, 2 * hidden + col : 2 * hidden + col + tile], preferred_element_type=f32
        )
        s = jax.nn.sigmoid(g)
        gs = g * s
        inner = gs * u
        scaled[e, rows, col : col + tile] = (inner * gate).astype(bf)
        grad_inner = raw * gate
        grad_act[e, rows, col : col + tile] = (grad_inner * u * s * (1.0 + g * (1.0 - s))).astype(bf)
        grad_act[e, rows, hidden + col : hidden + col + tile] = (grad_inner * gs).astype(bf)
        return jnp.sum(raw * inner, axis=1, keepdims=True)

    tile = min(256, hidden)
    found = {}

    def hidden_step(h, e, n):
        got = hidden_chunk(h, e, n, tile)
        found[(h, e)] = got if n == 0 else found[(h, e)] + got
        if n == hidden // tile - 1:
            gate_grad = found.pop((h, e))
            high = gate_grad.astype(bf).astype(f32)
            there = pl.ds(h * half, half)
            apart = (lane_id == EXPERT_COUNT + first + e).astype(f32)
            rows_buf[e, there, width:wide] = (high * here[e] + (gate_grad - high) * apart).astype(bf)

    def hidden_steps(h):
        return [functools.partial(hidden_step, h, e, n) for e in range(held) for n in range(hidden // tile)]

    def project(h, e, left, weight_cols):
        rows = pl.ds(h * half, half)
        lo, n = weight_cols
        for c0, cn in columns_of(width):
            rows_buf[e, rows, c0 : c0 + cn] = lax.dot_general(
                left[e, rows, :], weights[e, c0 : c0 + cn, lo : lo + n], (((1,), (1,)), ((), ())), preferred_element_type=f32
            ).astype(bf)

    def combine(target, h, k, cols):
        at = pl.ds(base_of(h, k), NY)
        r = row_of(h, k)
        for c0, cn in cols:
            parts = [rows_buf[e, r : r + pair, c0 : c0 + cn] for e in range(held)]
            if lanes > held * pair:
                parts.append(jnp.zeros((lanes - held * pair, cn), bf))
            got = jnp.dot(pick[h * NZ + k], jnp.concatenate(parts, axis=0), preferred_element_type=f32)
            target[at, :, c0 : c0 + cn] = got.astype(bf).reshape(NY, count, cn)

    stores = []

    def weight_grad(e, j):
        rows = pl.ds(pl.multiple_of((fsdp ^ j) * quarter, 128), quarter)
        slot = len(stores) % 2
        if len(stores) >= 2:
            stores[-2].wait()
        for c0, cn in columns_of(2 * hidden):
            stage[slot, :, c0 : c0 + cn] = lax.dot_general(
                taken[e, :, rows], grad_act[e, :, c0 : c0 + cn], (((0,), (0,)), ((), ())), preferred_element_type=f32
            ).astype(bf)
        stage[slot, :, 2 * hidden :] = lax.dot_general(
            cot_taken[e, :, rows], scaled[e], (((0,), (0,)), ((), ())), preferred_element_type=f32
        ).astype(bf)
        copy = pltpu.make_async_copy(stage.at[slot], grads[j].at[e], store_sem.at[len(stores)])
        copy.start()
        stores.append(copy)

    work = [functools.partial(cot_chunk, h, k) for h in range(NC) for k in range(NZ)]
    all_cols = columns_of(width) + [(width, 128)]
    ready = {(h, k): 0 for h in range(NC) for k in range(NZ)}
    ready[(0, 0)] = 1
    near_begun = False

    def wait_weights():
        for copy in loads:
            copy.wait()
        arrived = weights.at[held - 1, rows_of(fsdp ^ 3)]
        pltpu.make_async_remote_copy(
            src_ref=arrived, dst_ref=arrived, send_sem=piece_sem.at[0], recv_sem=piece_sem.at[1],
            device_id=there, device_id_type=DEV,
        ).wait_recv()

    for k, flips in gather_events(plans[0].order)[1:]:
        for way in ways:
            way.step(k, flips)
        key = (1 if C in flips else 0, k)
        ready[key] += 1
        if ready[key] == NY:
            work.append(functools.partial(dispatch, seen, taken, *key, all_cols))
            if all(ready[(g, n)] == NY for g in range(NC) for n in range(NZ // 2)) and not near_begun:
                near_begun = True
                work += [wait_weights] + hidden_steps(0)
        for _ in range(min(len(work), 1 if k < NZ - 1 else 2)):
            work.pop(0)()
    for chunk in work:
        chunk()
    for chunk in hidden_steps(1):
        chunk()

    far = list(reversed(range(NZ)))
    spare = spare_sem
    cut = lvl_b0.shape[2]
    in_ways = [
        Reduce(place, back[0], cot_seen.at[:, :, pl.ds(0, cut)], (lvl_b0, lvl_b1), chain_b, send_b, recv_b, spare),
        Reduce(place, back[1], cot_seen.at[:, :, pl.ds(cut, wide - cut)], (lvl_c0, lvl_c1), chain_c, send_c, recv_c, spare),
    ]
    in_steps = [step for t in range(NZ + 3) for way in in_ways for step in way.at_time(t)]
    for e in range(held):
        project(1, e, grad_act, (0, 2 * hidden))
    for k in far[: NZ // 2]:
        combine(cot_seen, 1, k, all_cols)
        for way in in_ways:
            way.first(k)
    for k in far[: NZ // 2]:
        combine(cot_seen, 0, k, all_cols)
    in_steps.pop(0)()
    in_steps.pop(0)()
    for e in range(held):
        project(0, e, grad_act, (0, 2 * hidden))
    in_steps.pop(0)()
    for k in far[NZ // 2 :]:
        combine(cot_seen, 1, k, all_cols)
        for way in in_ways:
            way.first(k)
    for _ in range(3):
        in_steps.pop(0)()
    for k in far[NZ // 2 :]:
        combine(cot_seen, 0, k, all_cols)
    for way in in_ways:
        way.level(0, 1)
        way.level(0, 0)
    done = ((0, 1), (0, 0))
    in_steps = [step for step in in_steps if not isinstance(step, functools.partial) or step.args not in done]
    for way in ways:
        way.finish()
    part_copies = []
    work = []

    def out_part(h, k):
        combine(seen, h, k, columns_of(width))
        at = pl.ds(base_of(h, k), NY)
        copy = pltpu.make_async_copy(seen.at[at, :, pl.ds(0, width)], part_out.at[at], part_sem.at[len(part_copies)])
        copy.start()
        part_copies.append(copy)

    for n in range(2):
        for e in range(held):
            work.append(functools.partial(project, n, e, scaled, (2 * hidden, hidden)))
        for k in range(n * NZ // 2, (n + 1) * NZ // 2):
            for h in range(NC):
                work.append(functools.partial(out_part, h, k))
    work += [functools.partial(weight_grad, e, j) for j in reversed(range(NX * NC)) for e in range(held)]
    while in_steps or work:
        if in_steps:
            in_steps.pop(0)()
        for _ in range(2):
            if work:
                work.pop(0)()
    in_ways[0].last(gin_out.at[:, pl.ds(0, cut)])
    in_ways[1].last(gin_out.at[:, pl.ds(cut, wide - cut)])
    piece.wait_send()
    for copy in stores[-2:] + part_copies:
        copy.wait()
    for way in in_ways:
        way.finish()


def moe(payload, cots, parts, cap, collective_id):
    count, wide = payload.shape
    width = wide - 128
    held, quarter, columns = parts[0].shape
    hidden = columns // 3
    cut = count * 3 // 4
    plans = [
        Plan(0, (Z, Y, C), (C, Z, Y), rows=(0, cut)),
        Plan(0, (Y, Z, C), (C, Z, Y), rows=(cut, count - cut)),
    ]
    back = [Plan(0, (C, Y, Z), (C, Z, Y)), Plan(0, (C, Z, Y), (C, Z, Y))]
    widths = (wide - wide // 4 // 128 * 128, wide // 4 // 128 * 128)
    blocks = NC * NZ * NY
    pair = NY * cap
    rows = blocks // NY * pair
    lanes = tile_up(held * pair, 128)
    bf, f32 = jnp.bfloat16, jnp.float32
    whole = pl.BlockSpec(memory_space=pltpu.VMEM)
    apart = pl.BlockSpec(memory_space=pl.ANY)
    dma = pltpu.SemaphoreType.DMA
    return pl.pallas_call(
        functools.partial(moe_kernel, plans, back, width, hidden, cap),
        out_shape=[
            jax.ShapeDtypeStruct((count, wide), f32),
            jax.ShapeDtypeStruct((blocks, count, width), bf),
        ]
        + [jax.ShapeDtypeStruct((held, quarter, columns), bf)] * (NX * NC),
        in_specs=[whole] + [apart] * 7,
        out_specs=[whole] + [apart] * (1 + NX * NC),
        scratch_shapes=[
            pltpu.VMEM((blocks, count, wide), bf),
            pltpu.VMEM((blocks, count, wide), bf),
            pltpu.VMEM((held, NX * NC * quarter, columns), bf),
            pltpu.VMEM((held, rows, wide), bf),
            pltpu.VMEM((held, rows, width), bf),
            pltpu.VMEM((held, rows, wide), bf),
            pltpu.VMEM((held, rows, hidden), bf),
            pltpu.VMEM((held, rows, 2 * hidden), bf),
            pltpu.VMEM((blocks // NY, NY * count, lanes), bf),
            pltpu.VMEM((2, quarter, columns), bf),
        ]
        + [pltpu.VMEM((n, count, w), bf) for p, w in zip(back, widths) for n in Reduce.counts(p)[0]]
        + [
            dma((sum(Gather.sends(p) for p in plans),)),
            dma((sum(p.blocks for p in plans),)),
            dma(()),
            *[dma((n,)) for p in back for n in Reduce.counts(p)[1:]],
            dma((held * NX * NC + blocks // NY,)),
            dma((held * NX * NC,)),
            dma((blocks // NY,)),
            dma((2,)),
        ],
        compiler_params=pltpu.CompilerParams(
            collective_id=collective_id, has_side_effects=True, vmem_limit_bytes=67043328
        ),
        name="experts",
    )(payload, cots, *parts)


def weights_kernel(plans, gain_at, *refs):
    left_one, right_one, left_two, right_two, left_small, right_small = refs[:6]
    matrix_in, hidden, gain, grad_mixed = refs[6:10]
    n_ways = len(plans)
    outs, grad_input = refs[10:13], refs[13]
    held = refs[14 : 14 + n_ways]
    buffers, refs = refs[14 + n_ways : 14 + 5 * n_ways], refs[14 + 5 * n_ways :]
    matrix, grad_in, halves = refs[:3]
    sems, (spare, matrix_sem) = refs[3 : 3 + 2 * n_ways], refs[3 + 2 * n_ways :]
    bf, f32 = jnp.bfloat16, jnp.float32
    place = Place()
    far = list(reversed(range(NZ)))
    fetch = pltpu.make_async_copy(matrix_in, matrix, matrix_sem)
    fetch.start()
    count_here = hail(place, (Z, Y, X, C))
    *ways, small_way = [
        Reduce(place, plan, held[n], buffers[4 * n : 4 * n + 3], buffers[4 * n + 3], sems[2 * n], sems[2 * n + 1], spare)
        for n, plan in enumerate(plans)
    ]
    group = NY * NX * NC
    rows = group * held[0].shape[1]

    def products(pairs, target, k, shift=0):
        at = pl.ds(pl.multiple_of(place.order[k] * rows, 128), rows)
        for c0, cn in columns_of(target.shape[2]):
            got = sum(
                lax.dot_general(
                    left[:, at], right[:, shift + c0 : shift + c0 + cn], (((0,), (0,)), ((), ())),
                    preferred_element_type=f32,
                )
                for left, right in pairs
            )
            target[pl.ds(place.order[k] * group, group), :, c0 : c0 + cn] = got.astype(target.dtype).reshape(
                group, rows // group, cn
            )

    def round_of(some, t):
        for way in some:
            for step in way.at_time(t):
                step()

    for t in range(NZ):
        for n, way in enumerate(ways):
            width = held[n].shape[2]
            products([(left_one, right_one) if n < 2 else (left_two, right_two)], held[n], far[t], n % 2 * width)
            if t == n == 0:
                meet(count_here)
            way.first(far[t])
        if t > 0:
            round_of(ways, t - 1)
    fetch.wait()
    for c0, cn in columns_of(grad_in.shape[1]):
        grad_in[:, c0 : c0 + cn] = lax.dot_general(
            right_one[...], matrix[c0 : c0 + cn], (((1,), (1,)), ((), ())), preferred_element_type=f32
        )
    count = grad_in.shape[0]
    wide = hidden[...].astype(f32)
    inverse = lax.rsqrt(jnp.mean(wide * wide, axis=1, keepdims=True) + norm_eps)
    unit = wide * inverse
    factor = grad_in[...] * unit
    high = factor.astype(bf)
    halves[:count] = high
    halves[count:] = (factor - high.astype(f32)).astype(bf)
    scaled = grad_in[...] * gain[...]
    mean = jnp.mean(scaled * unit, axis=1, keepdims=True)
    grad_input[...] = grad_mixed[...] + inverse * (scaled - unit * mean)
    column = (lax.broadcasted_iota(jnp.int32, (2 * count, 128), 1) == gain_at).astype(f32).astype(bf)
    for k in far:
        products([(left_small, right_small), (halves, column)], held[-1], k)
        small_way.first(k)
    late = [(0, 1, 2), (3, 4), (5,), (6,)]
    for n, t in enumerate(range(NZ - 1, NZ + 3)):
        round_of(ways, t)
        for t_small in late[n]:
            round_of([small_way], t_small)
    for n, way in enumerate(ways):
        width = held[n].shape[2]
        way.last(outs[n // 2].at[:, pl.ds(n % 2 * width, width)])
    small_way.last(outs[2])
    for way in ways + [small_way]:
        way.finish()


def return_weights(lefts, rights, matrix, hidden, gain, grad_mixed, gain_at, collective_id):
    width = lefts[0].shape[1]
    rows = width // (NZ * NY * NX * NC)
    widths = [r.shape[1] for r in rights]
    whole = (Z, Y, X, C)
    orders = ((C, Y, Z, X), (C, Y, Z, X), (C, X, Z, Y), (C, X, Y, Z), (C, Y, X, Z))
    plans = [Plan(0, order, whole) for order in orders]
    parts = [widths[0] // 2] * 2 + [widths[1] // 2] * 2 + [widths[2]]
    bf, f32 = jnp.bfloat16, jnp.float32
    dma = pltpu.SemaphoreType.DMA
    vmem = pl.BlockSpec(memory_space=pltpu.VMEM)
    count = hidden.shape[0]
    return pl.pallas_call(
        functools.partial(weights_kernel, plans, gain_at),
        out_shape=[jax.ShapeDtypeStruct((rows, w), f32) for w in widths] + [jax.ShapeDtypeStruct(hidden.shape, f32)],
        in_specs=[vmem] * 6 + [pl.BlockSpec(memory_space=pl.ANY)] + [vmem] * 3,
        out_specs=[vmem] * 4,
        scratch_shapes=[pltpu.VMEM((plans[0].blocks, rows, w), bf) for w in parts]
        + [pltpu.VMEM((n, rows, w), bf) for p, w in zip(plans, parts) for n in Reduce.counts(p)[0]]
        + [pltpu.VMEM(matrix.shape, bf), pltpu.VMEM(hidden.shape, f32), pltpu.VMEM((2 * count, width), bf)]
        + [dma((n,)) for p in plans for n in Reduce.counts(p)[1:]]
        + [dma(()), dma(())],
        compiler_params=pltpu.CompilerParams(
            collective_id=collective_id, has_side_effects=True, vmem_limit_bytes=64 * 1024 * 1024
        ),
        name="return_weights",
    )(*[a for pair in zip(lefts, rights) for a in pair], matrix, hidden, gain, grad_mixed)


def turn(block, cosine, sine):
    lane = lax.broadcasted_iota(jnp.int32, (1, 128), 1)
    half = HEAD_SIZE // 2
    other = jnp.where(lane % HEAD_SIZE < half, pltpu.roll(block, 128 - half, 1), pltpu.roll(block, half, 1))
    return block * cosine + other * sine


def place_heads(read, target, count):
    group = QUERY_HEADS // KEY_VALUE_HEADS
    lane = lax.broadcasted_iota(jnp.int32, (1, 2 * HEAD_SIZE), 1)
    for pair in range(QUERY_HEADS // 2):
        both = read(pair)
        for h in (2 * pair, 2 * pair + 1):
            m, g = h // group, h % group
            block = both if h % 2 == m % 2 else pltpu.roll(both, HEAD_SIZE, 1)
            block = jnp.where(lane // HEAD_SIZE == m % 2, block, 0.0)
            target[m, g * count : (g + 1) * count] = block.astype(target.dtype)


def collect_heads(source, target, count, finish):
    group = QUERY_HEADS // KEY_VALUE_HEADS
    lane = lax.broadcasted_iota(jnp.int32, (1, 2 * HEAD_SIZE), 1)
    for pair in range(QUERY_HEADS // 2):
        sides = []
        for h in (2 * pair, 2 * pair + 1):
            m, g = h // group, h % group
            block = source[m, g * count : (g + 1) * count]
            sides.append(block if h % 2 == m % 2 else pltpu.roll(block, HEAD_SIZE, 1))
        both = finish(jnp.where(lane < HEAD_SIZE, *sides))
        target[:, pair * 128 : pair * 128 + 128] = both.astype(target.dtype)


class Scores:
    def __init__(self, place, queries, keys):
        self.queries, self.keys = queries, keys
        group = QUERY_HEADS // KEY_VALUE_HEADS
        count = keys.shape[1]
        self.total = keys.shape[0] * count
        row = lax.broadcasted_iota(jnp.int32, (group * count, 1), 0) % count
        self.position = row + (place.at[Z] * NY + place.at[Y]) * count
        self.column = lax.broadcasted_iota(jnp.int32, (1, self.total), 1)

    def pair(self, m, shift):
        at = pl.ds(pl.multiple_of(shift + m // 2 * 128, 128), 128)
        return self.keys[:, :, at].reshape(self.total, 128)

    def of(self, m, keys):
        found = lax.dot_general(
            self.queries[m], keys, (((1,), (1,)), ((), ())), preferred_element_type=jnp.float32
        )
        return jnp.where(self.column <= self.position, found * attn_scale, masked_logits)


def attend_kernel(
    plans, linear, cot, routes, cosine, sine, out, log_sums, kv_out, cots, placed, seen, own_kv, own_cots, raw, *sems
):
    send_kv, recv_kv, send_cot, recv_cot, spare, own_sem = sems
    place = Place()
    bf, f32 = jnp.bfloat16, jnp.float32
    count_here = hail(place, (Z, Y, C))
    count = linear.shape[0]
    width = KEY_VALUE_HEADS * HEAD_SIZE
    q_width = QUERY_HEADS * HEAD_SIZE
    for c0 in range(0, width, 128):
        block = linear[:, q_width + c0 : q_width + c0 + 128]
        own_kv[:, c0 : c0 + 128] = turn(block, cosine[...], sine[...]).astype(bf)
    own_kv[:, width:] = linear[:, q_width + width :].astype(bf)
    model = cot.shape[1]
    own_cots[:, :model] = cot[...].astype(bf)
    expert = lax.broadcasted_iota(jnp.int32, (1, 128), 1)
    routed = routes[:, 0:1] == expert
    for n in range(1, routes.shape[1]):
        routed = jnp.logical_or(routed, routes[:, n : n + 1] == expert)
    own_cots[:, model:] = routed.astype(f32).astype(bf)
    meet(count_here)
    kv_way = Gather(place, plans[0], own_kv, seen, send_kv, recv_kv, spare, 0, 0)
    cot_ways, at = [], 0
    for n, plan in enumerate(plans[1:]):
        cot_ways.append(Gather(place, plan, own_cots, cots, send_cot, recv_cot, spare, at, n * plan.blocks))
        at += Gather.sends(plan)
    kv_way.step(0, ())
    for way in cot_ways:
        way.step(0, ())
    mine = pltpu.make_async_copy(own_cots, cots.at[flat_index(place.at, plans[1].index)], own_sem.at[0])
    mine.start()
    seen[flat_index(place.at, plans[0].index)] = own_kv[...]
    place_heads(lambda pair: turn(linear[:, pair * 128 : pair * 128 + 128], cosine[...], sine[...]), placed, count)
    log_sums[...] = jnp.zeros(log_sums.shape, f32)
    early = [e for e in gather_events(plans[1].order)[1:]]
    kv_events = gather_events(plans[0].order)[1:]
    for k, flips in kv_events:
        kv_way.step(k, flips)
        if len(early) > 8:
            event = early.pop(0)
            for way in cot_ways:
                way.step(*event)
    keep = pltpu.make_async_copy(seen, kv_out, own_sem.at[1])
    keep.start()
    scores = Scores(place, placed, seen)
    lane = lax.broadcasted_iota(jnp.int32, (1, 128), 1)

    def head(m, carry):
        for i in range(KEY_VALUE_HEADS):
            if early:
                event = early.pop(0)

                @pl.when(m == i)
                def _():
                    for way in cot_ways:
                        way.step(*event)

        s = scores.of(m, scores.pair(m, 0))
        best = jnp.max(s, axis=1, keepdims=True)
        weights = jnp.exp(s - best)
        total = jnp.sum(weights, axis=1, keepdims=True)
        mixed = jnp.dot(weights.astype(bf), scores.pair(m, width), preferred_element_type=f32)
        raw[m] = mixed / total
        log_sums[...] = jnp.where(lane == m, best + jnp.log(total), log_sums[...])
        return carry

    lax.fori_loop(0, KEY_VALUE_HEADS, head, 0)
    collect_heads(raw, out, count, lambda block: block)
    keep.wait()
    mine.wait()
    kv_way.finish()
    for way in cot_ways:
        way.finish()


def attend(linear, cot, routes, cosine, sine, collective_id):
    count = linear.shape[0]
    kv_width = 2 * KEY_VALUE_HEADS * HEAD_SIZE
    cut = count * 3 // 4
    plans = [
        Plan(0, (Z, Y), (Z, Y)),
        Plan(1, (Z, Y, C), (C, Z, Y), rows=(0, cut)),
        Plan(1, (Y, Z, C), (C, Z, Y), rows=(cut, count - cut)),
    ]
    bf, f32 = jnp.bfloat16, jnp.float32
    group = QUERY_HEADS // KEY_VALUE_HEADS
    vmem = pl.BlockSpec(memory_space=pltpu.VMEM)
    apart = pl.BlockSpec(memory_space=pl.ANY)
    dma = pltpu.SemaphoreType.DMA
    kv_shape = (plans[0].blocks, count, kv_width)
    cot_shape = (count, cot.shape[1] + 128)
    heads = (KEY_VALUE_HEADS, group * count, 2 * HEAD_SIZE)
    return pl.pallas_call(
        functools.partial(attend_kernel, plans),
        out_shape=[
            jax.ShapeDtypeStruct((count, QUERY_HEADS * HEAD_SIZE), bf),
            jax.ShapeDtypeStruct((group * count, 128), f32),
            jax.ShapeDtypeStruct(kv_shape, bf),
            jax.ShapeDtypeStruct((plans[1].blocks,) + cot_shape, bf),
            jax.ShapeDtypeStruct(heads, bf),
        ],
        in_specs=[vmem] * 5,
        out_specs=[vmem, vmem, apart, apart, vmem],
        scratch_shapes=[
            pltpu.VMEM(kv_shape, bf),
            pltpu.VMEM((count, kv_width), bf),
            pltpu.VMEM(cot_shape, bf),
            pltpu.VMEM(heads, f32),
        ]
        + [
            dma((Gather.sends(plans[0]),)),
            dma((plans[0].blocks,)),
            dma((Gather.sends(plans[1]) + Gather.sends(plans[2]),)),
            dma((plans[1].blocks + plans[2].blocks,)),
            dma(()),
            dma((2,)),
        ],
        compiler_params=pltpu.CompilerParams(
            collective_id=collective_id, has_side_effects=True, vmem_limit_bytes=56 * 1024 * 1024
        ),
        name="attend",
    )(linear, cot, routes, cosine, sine)


def attend_back_kernel(plans, *refs):
    placed, gin, gate_map, cot, ffn_gain, outputs, log_sums, keys, part, w_o, mixed, cosine, sine = refs[:13]
    back, layer_out, grad_mixed, grad_attn, left_small, right_small = refs[13:19]
    kv_grad, grads_placed, raw, deltas, held, held_out, grads, matrix = refs[19:27]
    level, chain, v_level, v_chain, out_level, out_level_two, out_chain = refs[27:34]
    send_kv, recv_kv, send_v, recv_v, send_out, recv_out, spare, load_sem, matrix_sem = refs[34:]
    place = Place()
    bf, f32 = jnp.bfloat16, jnp.float32
    far = list(reversed(range(NZ)))
    loads = []
    for k in far:
        for h in (1 - place.at[C], place.at[C]):
            at = pl.ds((h * NZ + place.order[k]) * NY, NY)
            loads.append(pltpu.make_async_copy(part.at[at], held_out.at[at], load_sem.at[len(loads)]))
    for copy in loads:
        copy.start()
    fetch = pltpu.make_async_copy(w_o, matrix, matrix_sem)
    fetch.start()
    meet(hail(place, (Z, Y, C)))
    width = KEY_VALUE_HEADS * HEAD_SIZE
    k_way = Reduce(place, plans[0], held.at[:, :, pl.ds(0, width)], (level,), chain, send_kv, recv_kv, spare)
    v_way = Reduce(place, plans[1], held.at[:, :, pl.ds(width, width)], (v_level,), v_chain, send_v, recv_v, spare)
    out_way = Reduce(place, plans[2], held_out, (out_level, out_level_two), out_chain, send_out, recv_out, spare)
    for copy in loads:
        copy.wait()
    for k in far:
        out_way.first(k)
    count = grads.shape[0]
    fetch.wait()
    out_way.level(0, 3)
    out_way.level(0, 2)
    model = cot.shape[1]
    lane = lax.broadcasted_iota(jnp.int32, (1, 128), 1)
    halves = gin[:, model:]
    gate_grad = jnp.where(lane < EXPERT_COUNT, halves + pltpu.roll(halves, 128 - EXPERT_COUNT, 1), 0.0)
    weighted = jnp.sum(gate_map[...] * gate_grad, axis=1, keepdims=True)
    grad_logits = (gate_map[...] * (gate_grad - weighted)).astype(bf)
    over_cols = (((1,), (1,)), ((), ()))
    inverse = lax.rsqrt(jnp.mean(mixed[...] * mixed[...], axis=1, keepdims=True) + norm_eps)
    unit = mixed[...] * inverse
    grad_in = gin[:, :model] + lax.dot_general(
        grad_logits, matrix[:, model:], over_cols, preferred_element_type=f32
    )
    scaled = grad_in * ffn_gain[...]
    grad_mixed[...] = cot[...] + inverse * (scaled - unit * jnp.mean(scaled * unit, axis=1, keepdims=True))
    grad_attn[...] = grad_mixed[...].astype(bf)
    factor = grad_in * unit
    high = factor.astype(bf)
    left_small[:count] = (unit * ffn_gain[...]).astype(bf)
    left_small[count : 2 * count] = high
    left_small[2 * count :] = (factor - high.astype(f32)).astype(bf)
    right_small[:count] = grad_logits
    right_small[count:] = jnp.broadcast_to(jnp.where(lane == EXPERT_COUNT + 1, 1.0, 0.0), (2 * count, 128)).astype(bf)
    for c0, cn in columns_of(grads.shape[1]):
        grads[:, c0 : c0 + cn] = lax.dot_general(
            grad_attn[...], matrix[c0 : c0 + cn, :model], over_cols, preferred_element_type=f32
        ).astype(bf)
    out_way.level(0, 1)
    place_heads(lambda pair: grads[:, pair * 128 : pair * 128 + 128].astype(f32), grads_placed, count)
    group = QUERY_HEADS // KEY_VALUE_HEADS
    lane = lax.broadcasted_iota(jnp.int32, (1, 128), 1)
    for g in range(group):
        found = jnp.zeros((count, 128), f32)
        for m in range(KEY_VALUE_HEADS):
            h = m * group + g
            at = slice(h // 2 * 128, h // 2 * 128 + 128)
            both = grads[:, at].astype(f32) * outputs[:, at].astype(f32)
            delta = jnp.sum(jnp.where(lane // HEAD_SIZE == h % 2, both, 0.0), axis=1, keepdims=True)
            found = jnp.where(lane == m, delta, found)
        deltas[g * count : (g + 1) * count] = found
    scores = Scores(place, placed, keys)
    blocks = keys.shape[0]
    turns = KEY_VALUE_HEADS // 2
    early = [[(out_way.level, 1, 3)], [(out_way.along, 3), (out_way.level, 1, 2)], [(out_way.along, 2)], []]

    def pair(p, carry):
        for i in range(turns):

            @pl.when(p == i)
            def _():
                for step, *at in early[i]:
                    step(*at)

        key_sum = value_sum = None
        for side in range(2):
            m = 2 * p + side
            k_pair, v_pair = scores.pair(m, 0), scores.pair(m, width)
            of_head = lambda ref: jnp.sum(jnp.where(lane == m, ref[...], 0.0), axis=1, keepdims=True)
            weights = jnp.exp(scores.of(m, k_pair) - of_head(log_sums))
            grad = grads_placed[m]
            grad_probs = lax.dot_general(grad, v_pair, (((1,), (1,)), ((), ())), preferred_element_type=f32)
            grad_scores = (weights * (grad_probs - of_head(deltas))).astype(bf)
            raw[m] = attn_scale * jnp.dot(grad_scores, k_pair, preferred_element_type=f32)
            over_rows = (((0,), (0,)), ((), ()))
            key_part = lax.dot_general(grad_scores, placed[m], over_rows, preferred_element_type=f32)
            value_part = lax.dot_general(weights.astype(bf), grad, over_rows, preferred_element_type=f32)
            key_sum = key_part if key_sum is None else key_sum + key_part
            value_sum = value_part if value_sum is None else value_sum + value_part
        at = pl.multiple_of(p * 128, 128)
        held[:, :, pl.ds(at, 128)] = (attn_scale * key_sum).astype(bf).reshape(blocks, count, 128)
        at = pl.multiple_of(width + p * 128, 128)
        held[:, :, pl.ds(at, 128)] = value_sum.astype(bf).reshape(blocks, count, 128)
        return carry

    lax.fori_loop(0, turns, pair, 0)
    for k in far:
        k_way.first(k)
    v_way.along(3)
    out_way.level(0, 0)
    collect_heads(raw, back, count, lambda block: turn(block, cosine[...], -sine[...]))
    k_way.level(0, 3)
    v_way.along(2)
    k_way.level(0, 2)
    k_way.along(3)
    v_way.along(1)
    k_way.level(0, 1)
    k_way.along(2)
    v_way.settle()
    k_way.level(0, 0)
    k_way.along(1)
    k_way.last(kv_grad.at[:, pl.ds(0, width)])
    v_way.level(1, 0)
    v_way.last(kv_grad.at[:, pl.ds(width, width)])
    q_width = QUERY_HEADS * HEAD_SIZE
    for c0 in range(0, width, 128):
        block = turn(kv_grad[:, c0 : c0 + 128], cosine[...], -sine[...])
        back[:, q_width + c0 : q_width + c0 + 128] = block.astype(bf)
    back[:, q_width + width :] = kv_grad[:, width:].astype(bf)
    out_way.level(1, 1)
    out_way.along(1)
    out_way.level(1, 0)
    out_way.last(layer_out, mixed)
    for way in (k_way, v_way, out_way):
        way.finish()


def attend_back(
    placed, gin, gate_map, cot, ffn_gain, outputs, log_sums, keys, part, w_o, mixed, cosine, sine, collective_id
):
    count, kv_width = keys.shape[1:]
    plans = [Plan(0, (Y, Z), (Z, Y)), Plan(0, (Z, Y), (Z, Y)), Plan(1, (C, Y, Z), (C, Z, Y))]
    bf, f32 = jnp.bfloat16, jnp.float32
    group = QUERY_HEADS // KEY_VALUE_HEADS
    vmem = pl.BlockSpec(memory_space=pltpu.VMEM)
    apart = pl.BlockSpec(memory_space=pl.ANY)
    dma = pltpu.SemaphoreType.DMA
    heads = (KEY_VALUE_HEADS, group * count, 2 * HEAD_SIZE)
    blocks = [(count, kv_width // 2)] * 2 + [part.shape[1:]]
    return pl.pallas_call(
        functools.partial(attend_back_kernel, plans),
        out_shape=[
            jax.ShapeDtypeStruct((count, outputs.shape[1] + kv_width), bf),
            jax.ShapeDtypeStruct(mixed.shape, bf),
            jax.ShapeDtypeStruct(mixed.shape, f32),
            jax.ShapeDtypeStruct(mixed.shape, bf),
            jax.ShapeDtypeStruct((3 * count, mixed.shape[1]), bf),
            jax.ShapeDtypeStruct((3 * count, 128), bf),
        ],
        in_specs=[vmem] * 8 + [apart] * 2 + [vmem] * 3,
        out_specs=[vmem] * 6,
        scratch_shapes=[
            pltpu.VMEM((count, kv_width), f32),
            pltpu.VMEM(heads, bf),
            pltpu.VMEM(heads, f32),
            pltpu.VMEM((group * count, 128), f32),
            pltpu.VMEM(keys.shape, bf),
            pltpu.VMEM(part.shape, bf),
            pltpu.VMEM(outputs.shape, bf),
            pltpu.VMEM(w_o.shape, bf),
        ]
        + [pltpu.VMEM((n,) + b, bf) for p, b in zip(plans, blocks) for n in Reduce.counts(p)[0]]
        + [dma((n,)) for p in plans for n in Reduce.counts(p)[1:]]
        + [dma(()), dma((NC * NZ,)), dma(())],
        compiler_params=pltpu.CompilerParams(
            collective_id=collective_id, has_side_effects=True, vmem_limit_bytes=64 * 1024 * 1024
        ),
        name="attend_back",
    )(placed, gin, gate_map, cot, ffn_gain, outputs, log_sums, keys, part, w_o, mixed, cosine, sine)


def last_kernel(core_ref, own, core_part, x_part, both_part, one, two, small, layer, grad, *outs):
    core = core_ref[0]
    in_out, out_out = outs[:2]
    split = in_out.shape[3]
    for at, left, right in ((core, own, x_part), (1 - core, core_part, both_part)):
        total = left[0].astype(jnp.float32) + right[0].astype(jnp.float32)
        in_out[at, 0] = total[:, :split]
        out_out[at, 0] = total[:, split:]

    @pl.when(jnp.logical_and(pl.program_id(0) == 0, pl.program_id(1) == 0))
    def _():
        wq, wk, wv, wo, router, first_gain, second_gain, layer_out, grad_out = outs[2:]
        layer_out[...] = layer[...]
        grad_out[...] = grad[...]
        q, k = wq.shape[1], wk.shape[1]
        wq[...] = one[:, :q]
        wk[...] = one[:, q : q + k]
        wv[...] = one[:, q + k :]
        wo[...] = two[...]
        turned = small[...].T
        at = router.shape[0]
        router[...] = turned[:at]
        first_gain[...] = turned[at : at + 1]
        second_gain[...] = turned[at + 1 : at + 2]


def last_outputs(pieces, core, split, sums, widths):
    held, quarter, columns = pieces[0].shape
    step = quarter // 2
    rows = sums[0].shape[0]
    spec = pl.BlockSpec((1, step, columns), lambda e, r, c: (e, r, 0))
    fixed = lambda a, b: pl.BlockSpec((a, b), lambda e, r, c: (0, 0))
    outs = (split, columns - split)
    shapes = [(rows, w) for w in widths[:-1]] + [(widths[-1], rows)] + [(1, rows)] * 2 + [a.shape for a in sums[3:]]
    types = [jnp.float32] * 7 + [a.dtype for a in sums[3:]]
    return pl.pallas_call(
        last_kernel,
        grid_spec=pltpu.PrefetchScalarGridSpec(
            num_scalar_prefetch=1,
            grid=(held, 2),
            in_specs=[spec] * 4 + [fixed(*a.shape) for a in sums],
            out_specs=[pl.BlockSpec((NC, 1, step, w), lambda e, r, c: (0, e, r, 0)) for w in outs]
            + [fixed(*s) for s in shapes],
        ),
        out_shape=[jax.ShapeDtypeStruct((NC, held, quarter, w), jnp.float32) for w in outs]
        + [jax.ShapeDtypeStruct(s, d) for s, d in zip(shapes, types)],
        name="last_outputs",
    )(core[None], *pieces, *sums)


MODEL_WIDTH = 1536
QUERY_HEADS = 24
KEY_VALUE_HEADS = 8
HEAD_SIZE = 64
EXPERT_HIDDEN = 512
EXPERT_COUNT = 32
TOP = 8
CAP = 40


norm_eps = 1e-06
attn_scale = 0.015625
rope_base = 10000.0
masked_logits = -1e30


def rope_tables(positions):
    half = HEAD_SIZE // 2
    frequency = jnp.power(
        jnp.float32(rope_base), -2.0 * jnp.arange(half, dtype=jnp.float32) / HEAD_SIZE
    )
    angle = positions.astype(jnp.float32)[:, None] * frequency[None, :]
    return (jnp.cos(angle)[:, None, :], jnp.sin(angle)[:, None, :])


def rotate_pairs(value_tensor, cosine_table, sine_table):
    half = value_tensor.shape[-1] // 2
    first = value_tensor[..., :half]
    second = value_tensor[..., half:]
    return jnp.concatenate(
        [first * cosine_table - second * sine_table, second * cosine_table + first * sine_table],
        axis=-1,
    )


def rms_forward(wide, gain):
    inverse = lax.rsqrt(jnp.mean(wide * wide, axis=-1, keepdims=True) + norm_eps)
    unit = wide * inverse
    return (unit, inverse, (unit * gain.astype(jnp.float32)).astype(jnp.bfloat16))


def rms_backward(grad, unit, inverse, gain):
    scaled = grad * gain.astype(jnp.float32)
    back = inverse * (scaled - unit * jnp.mean(scaled * unit, axis=-1, keepdims=True))
    return (back, jnp.sum(grad * unit, axis=0))


def piece_scores(query_rows, key_section, positions):
    token_count = key_section.shape[0]
    key_tensor = key_section.reshape(token_count, KEY_VALUE_HEADS, HEAD_SIZE)
    scores = (
        jnp.einsum("tkgd,nkd->kgtn", query_rows, key_tensor, preferred_element_type=jnp.float32)
        * attn_scale
    )
    visible = jnp.arange(token_count, dtype=jnp.int32)[None, :] <= positions[:, None]
    return (jnp.where(visible, scores, masked_logits), visible, key_tensor)


def local(
    hidden,
    routes,
    attn_norm,
    ffn_norm,
    w_q,
    key_weight,
    value_weight,
    w_o,
    router,
    expert_in,
    expert_out,
    cotangent,
):
    token_rows = hidden.shape[1]
    query_group = QUERY_HEADS // KEY_VALUE_HEADS
    ctx_size = lax.axis_size(CTX)
    sequence_length = token_rows * ctx_size
    positions = lax.axis_index(CTX) * token_rows + jnp.arange(token_rows, dtype=jnp.int32)
    cosine_table, sine_table = rope_tables(positions)
    contract_rows = (((0,), (0,)), ((), ()))
    contract_cols = (((1,), (1,)), ((), ()))
    layer = (
        lax.all_gather(attn_norm, (CTX, FSDP), axis=0, tiled=True),
        lax.all_gather(ffn_norm, (CTX, FSDP), axis=0, tiled=True),
        lax.all_gather(w_q, (CTX, FSDP), axis=0, tiled=True),
        lax.all_gather(key_weight, (CTX, FSDP), axis=0, tiled=True),
        lax.all_gather(value_weight, (CTX, FSDP), axis=0, tiled=True),
        lax.all_gather(w_o, (CTX, FSDP), axis=0, tiled=True),
        lax.all_gather(router, (CTX, FSDP), axis=0, tiled=True),
    )
    attn_gain, ffn_gain, query_w, key_weight_matrix, value_w, output_w, router_w = layer
    experts = (
        lax.all_gather(expert_in, FSDP, axis=1, tiled=True),
        lax.all_gather(expert_out, FSDP, axis=1, tiled=True),
    )
    weight_in, weight_out = experts
    wide = hidden[0].astype(jnp.float32)
    attn_unit, inverse_one, attention_input = rms_forward(wide, attn_gain)
    query_linear = jnp.dot(attention_input, query_w, preferred_element_type=jnp.float32).reshape(
        token_rows, QUERY_HEADS, HEAD_SIZE
    )
    query_rows = (
        rotate_pairs(query_linear, cosine_table, sine_table)
        .astype(jnp.bfloat16)
        .reshape(token_rows, KEY_VALUE_HEADS, query_group, HEAD_SIZE)
    )
    key_linear = jnp.dot(
        attention_input, key_weight_matrix, preferred_element_type=jnp.float32
    ).reshape(token_rows, KEY_VALUE_HEADS, HEAD_SIZE)
    key_matrix_rows = (
        rotate_pairs(key_linear, cosine_table, sine_table)
        .astype(jnp.bfloat16)
        .reshape(token_rows, KEY_VALUE_HEADS * HEAD_SIZE)
    )
    value_rows = jnp.dot(attention_input, value_w, preferred_element_type=jnp.float32).astype(
        jnp.bfloat16
    )
    init_state = (
        jnp.full((KEY_VALUE_HEADS, query_group, token_rows), masked_logits, jnp.float32),
        jnp.zeros((KEY_VALUE_HEADS, query_group, token_rows), jnp.float32),
        jnp.zeros((KEY_VALUE_HEADS, query_group, token_rows, HEAD_SIZE), jnp.float32),
    )
    key_section = lax.all_gather(key_matrix_rows, CTX, axis=0, tiled=True)
    value_section = lax.all_gather(value_rows, CTX, axis=0, tiled=True)

    def compute(current):
        best, total, weighted = current
        scores, visible, _ = piece_scores(query_rows, key_section, positions)
        value_tensor = value_section.reshape(value_section.shape[0], KEY_VALUE_HEADS, HEAD_SIZE)
        new_best = jnp.maximum(best, jnp.max(scores, axis=-1))
        weights = jnp.where(visible, jnp.exp(scores - new_best[..., None]), 0.0)
        total = jnp.sum(weights, axis=-1)
        weighted = jnp.einsum(
            "kgtn,nkd->kgtd",
            weights.astype(jnp.bfloat16),
            value_tensor,
            preferred_element_type=jnp.float32,
        )
        return (new_best, total, weighted)

    best, total, weighted = lax.cond(
        jnp.int32(0) <= positions[-1], compute, lambda current: current, init_state
    )
    log_sum_rows = best + jnp.log(total)
    attention_output = (
        jnp.transpose(weighted / total[..., None], (2, 0, 1, 3))
        .reshape(token_rows, QUERY_HEADS * HEAD_SIZE)
        .astype(jnp.bfloat16)
    )
    mixed = wide + jnp.dot(attention_output, output_w, preferred_element_type=jnp.float32)
    ffn_unit, inverse_two, ffn_in = rms_forward(mixed, ffn_gain)
    logits = jnp.dot(ffn_in, router_w, preferred_element_type=jnp.float32)
    route = routes[0]
    indicator = (route[:, :, None] == jnp.arange(EXPERT_COUNT, dtype=jnp.int32)).astype(jnp.float32)
    chosen = jnp.sum(indicator * logits[:, None, :], axis=-1)
    gates = jax.nn.softmax(chosen, axis=-1)
    flat_route = route.reshape(-1)
    counter = (flat_route[:, None] == jnp.arange(EXPERT_COUNT, dtype=jnp.int32)).astype(jnp.int32)
    slot = jnp.sum(counter * (jnp.cumsum(counter, axis=0) - 1), axis=1)
    target = flat_route * CAP + slot
    owner = (
        jnp.full((EXPERT_COUNT * CAP,), token_rows * TOP, jnp.int32)
        .at[target]
        .set(jnp.arange(token_rows * TOP, dtype=jnp.int32))
    )
    ffn_pad = jnp.concatenate([ffn_in, jnp.zeros((1, MODEL_WIDTH), jnp.bfloat16)], axis=0)
    local_experts = weight_in.shape[0]
    outgoing = ffn_pad[owner // TOP].reshape(ctx_size, local_experts, CAP, MODEL_WIDTH)
    received = lax.all_to_all(outgoing, CTX, split_axis=0, concat_axis=2, tiled=True)[0]
    act = jnp.einsum("erd,edf->erf", received, weight_in, preferred_element_type=jnp.float32)
    gate_part = act[..., :EXPERT_HIDDEN]
    up_part = act[..., EXPERT_HIDDEN:]
    sigma = jax.nn.sigmoid(gate_part)
    inner = (gate_part * sigma * up_part).astype(jnp.bfloat16)
    produced = jnp.einsum(
        "erf,edf->erd", inner, weight_out, preferred_element_type=jnp.float32
    ).astype(jnp.bfloat16)
    returned = lax.all_to_all(
        produced[None], CTX, split_axis=2, concat_axis=0, tiled=True
    ).reshape(EXPERT_COUNT * CAP, MODEL_WIDTH)
    picked = returned[target].reshape(token_rows, TOP, MODEL_WIDTH)
    layer_out = (mixed + jnp.sum(gates[..., None] * picked, axis=1)).astype(jnp.bfloat16)
    cot = cotangent[0]
    layer = (
        lax.all_gather(attn_norm, (CTX, FSDP), axis=0, tiled=True),
        lax.all_gather(ffn_norm, (CTX, FSDP), axis=0, tiled=True),
        lax.all_gather(w_q, (CTX, FSDP), axis=0, tiled=True),
        lax.all_gather(key_weight, (CTX, FSDP), axis=0, tiled=True),
        lax.all_gather(value_weight, (CTX, FSDP), axis=0, tiled=True),
        lax.all_gather(w_o, (CTX, FSDP), axis=0, tiled=True),
        lax.all_gather(router, (CTX, FSDP), axis=0, tiled=True),
    )
    attn_gain, ffn_gain, query_w, key_weight_matrix, value_w, output_w, router_w = layer
    experts = (
        lax.all_gather(expert_in, FSDP, axis=1, tiled=True),
        lax.all_gather(expert_out, FSDP, axis=1, tiled=True),
    )
    weight_in, weight_out = experts
    grad_gate = jnp.sum(cot[:, None, :] * picked, axis=-1)
    slot_grads = (
        (gates[..., None] * cot[:, None, :])
        .astype(jnp.bfloat16)
        .reshape(token_rows * TOP, MODEL_WIDTH)
    )
    slot_pad = jnp.concatenate([slot_grads, jnp.zeros((1, MODEL_WIDTH), jnp.bfloat16)], axis=0)
    grad_outgoing = slot_pad[owner].reshape(ctx_size, local_experts, CAP, MODEL_WIDTH)
    grad_received = lax.all_to_all(grad_outgoing, CTX, split_axis=0, concat_axis=2, tiled=True)[0]
    grad_w_out = jnp.einsum(
        "erd,erf->edf", grad_received, inner, preferred_element_type=jnp.float32
    )
    grad_inner = jnp.einsum(
        "erd,edf->erf", grad_received, weight_out, preferred_element_type=jnp.float32
    )
    grad_act = jnp.concatenate(
        [
            grad_inner * up_part * sigma * (1.0 + gate_part * (1.0 - sigma)),
            grad_inner * gate_part * sigma,
        ],
        axis=-1,
    ).astype(jnp.bfloat16)
    grad_w_in = jnp.einsum("erd,erf->edf", received, grad_act, preferred_element_type=jnp.float32)
    grad_rows = jnp.einsum(
        "erf,edf->erd", grad_act, weight_in, preferred_element_type=jnp.float32
    ).astype(jnp.bfloat16)
    grad_back = lax.all_to_all(
        grad_rows[None], CTX, split_axis=2, concat_axis=0, tiled=True
    ).reshape(EXPERT_COUNT * CAP, MODEL_WIDTH)
    grad_expert_in, grad_expert_out = (
        lax.psum_scatter(
            grad_w_in.astype(jnp.bfloat16), FSDP, scatter_dimension=1, tiled=True
        ).astype(jnp.float32),
        lax.psum_scatter(
            grad_w_out.astype(jnp.bfloat16), FSDP, scatter_dimension=1, tiled=True
        ).astype(jnp.float32),
    )
    grad_chosen = gates * (grad_gate - jnp.sum(gates * grad_gate, axis=-1, keepdims=True))
    grad_logits = jnp.sum(indicator * grad_chosen[..., None], axis=1).astype(jnp.bfloat16)
    grad_router_part = lax.dot_general(
        ffn_in, grad_logits, contract_rows, preferred_element_type=jnp.float32
    )
    grad_ffn_in = lax.dot_general(
        grad_logits, router_w, contract_cols, preferred_element_type=jnp.float32
    )
    grad_ffn_in = grad_ffn_in + jnp.sum(
        grad_back[target].reshape(token_rows, TOP, MODEL_WIDTH), axis=1, dtype=jnp.float32
    )
    back_two, grad_ffn_gain = rms_backward(grad_ffn_in, ffn_unit, inverse_two, ffn_gain)
    grad_mixed = cot + back_two
    grad_attn = grad_mixed.astype(jnp.bfloat16)
    grad_wo_part = lax.dot_general(
        attention_output, grad_attn, contract_rows, preferred_element_type=jnp.float32
    )
    attention_output_gradient = lax.dot_general(
        grad_attn, output_w, contract_cols, preferred_element_type=jnp.float32
    ).astype(jnp.bfloat16)
    head_gradient = attention_output_gradient.reshape(
        token_rows, KEY_VALUE_HEADS, query_group, HEAD_SIZE
    )
    delta_rows = jnp.sum(
        head_gradient.astype(jnp.float32)
        * attention_output.reshape(token_rows, KEY_VALUE_HEADS, query_group, HEAD_SIZE).astype(
            jnp.float32
        ),
        axis=-1,
    )
    delta_rows = jnp.transpose(delta_rows, (1, 2, 0))
    init_back = (
        jnp.zeros((token_rows, KEY_VALUE_HEADS, query_group, HEAD_SIZE), jnp.float32),
        jnp.zeros((sequence_length, 2 * KEY_VALUE_HEADS * HEAD_SIZE), jnp.float32),
    )
    attend_key_section = lax.all_gather(key_matrix_rows, CTX, axis=0, tiled=True)
    attend_value_section = lax.all_gather(value_rows, CTX, axis=0, tiled=True)

    def compute(current):
        token_count = attend_key_section.shape[0]
        scores, visible, key_tensor = piece_scores(query_rows, attend_key_section, positions)
        value_tensor = attend_value_section.reshape(token_count, KEY_VALUE_HEADS, HEAD_SIZE)
        weights_full = jnp.where(visible, jnp.exp(scores - log_sum_rows[..., None]), 0.0)
        grad_probs = jnp.einsum(
            "tkgd,nkd->kgtn", head_gradient, value_tensor, preferred_element_type=jnp.float32
        )
        grad_scores = (weights_full * (grad_probs - delta_rows[..., None])).astype(jnp.bfloat16)
        grad_query = attn_scale * jnp.einsum(
            "kgtn,nkd->tkgd", grad_scores, key_tensor, preferred_element_type=jnp.float32
        )
        key_portion = attn_scale * jnp.einsum(
            "kgtn,tkgd->nkd", grad_scores, query_rows, preferred_element_type=jnp.float32
        )
        value_portion = jnp.einsum(
            "kgtn,tkgd->nkd",
            weights_full.astype(jnp.bfloat16),
            head_gradient,
            preferred_element_type=jnp.float32,
        )
        update = jnp.concatenate(
            [
                key_portion.reshape(token_count, KEY_VALUE_HEADS * HEAD_SIZE),
                value_portion.reshape(token_count, KEY_VALUE_HEADS * HEAD_SIZE),
            ],
            axis=1,
        )
        return (grad_query, update)

    grad_query, grad_keys_full = lax.cond(
        jnp.int32(0) <= positions[-1], compute, lambda current: current, init_back
    )
    local_gradients = lax.psum_scatter(
        grad_keys_full.astype(jnp.bfloat16), CTX, scatter_dimension=0, tiled=True
    ).astype(jnp.float32)
    query_back = (
        rotate_pairs(
            grad_query.reshape(token_rows, QUERY_HEADS, HEAD_SIZE), cosine_table, -sine_table
        )
        .astype(jnp.bfloat16)
        .reshape(token_rows, QUERY_HEADS * HEAD_SIZE)
    )
    key_backward_rows = (
        rotate_pairs(
            local_gradients[:, : KEY_VALUE_HEADS * HEAD_SIZE].reshape(
                token_rows, KEY_VALUE_HEADS, HEAD_SIZE
            ),
            cosine_table,
            -sine_table,
        )
        .astype(jnp.bfloat16)
        .reshape(token_rows, KEY_VALUE_HEADS * HEAD_SIZE)
    )
    value_backward_rows = local_gradients[:, KEY_VALUE_HEADS * HEAD_SIZE :].astype(jnp.bfloat16)
    grad_wq_part = lax.dot_general(
        attention_input, query_back, contract_rows, preferred_element_type=jnp.float32
    )
    grad_wk_part = lax.dot_general(
        attention_input, key_backward_rows, contract_rows, preferred_element_type=jnp.float32
    )
    grad_wv_part = lax.dot_general(
        attention_input, value_backward_rows, contract_rows, preferred_element_type=jnp.float32
    )
    grad_attn_in = lax.dot_general(
        query_back, query_w, contract_cols, preferred_element_type=jnp.float32
    )
    grad_attn_in = grad_attn_in + lax.dot_general(
        key_backward_rows, key_weight_matrix, contract_cols, preferred_element_type=jnp.float32
    )
    grad_attn_in = grad_attn_in + lax.dot_general(
        value_backward_rows, value_w, contract_cols, preferred_element_type=jnp.float32
    )
    back_one, grad_attn_gain = rms_backward(grad_attn_in, attn_unit, inverse_one, attn_gain)
    grad_input = grad_mixed + back_one
    partial_sums = (
        lax.psum_scatter(
            grad_attn_gain.astype(jnp.bfloat16), CTX, scatter_dimension=0, tiled=True
        ).astype(jnp.float32),
        lax.psum_scatter(
            grad_ffn_gain.astype(jnp.bfloat16), CTX, scatter_dimension=0, tiled=True
        ).astype(jnp.float32),
        lax.psum_scatter(
            grad_wq_part.astype(jnp.bfloat16), CTX, scatter_dimension=0, tiled=True
        ).astype(jnp.float32),
        lax.psum_scatter(
            grad_wk_part.astype(jnp.bfloat16), CTX, scatter_dimension=0, tiled=True
        ).astype(jnp.float32),
        lax.psum_scatter(
            grad_wv_part.astype(jnp.bfloat16), CTX, scatter_dimension=0, tiled=True
        ).astype(jnp.float32),
        lax.psum_scatter(
            grad_wo_part.astype(jnp.bfloat16), CTX, scatter_dimension=0, tiled=True
        ).astype(jnp.float32),
        lax.psum_scatter(
            grad_router_part.astype(jnp.bfloat16), CTX, scatter_dimension=0, tiled=True
        ).astype(jnp.float32),
    )
    summed = (
        lax.psum_scatter(
            partial_sums[0].astype(jnp.bfloat16), FSDP, scatter_dimension=0, tiled=True
        ).astype(jnp.float32),
        lax.psum_scatter(
            partial_sums[1].astype(jnp.bfloat16), FSDP, scatter_dimension=0, tiled=True
        ).astype(jnp.float32),
        lax.psum_scatter(
            partial_sums[2].astype(jnp.bfloat16), FSDP, scatter_dimension=0, tiled=True
        ).astype(jnp.float32),
        lax.psum_scatter(
            partial_sums[3].astype(jnp.bfloat16), FSDP, scatter_dimension=0, tiled=True
        ).astype(jnp.float32),
        lax.psum_scatter(
            partial_sums[4].astype(jnp.bfloat16), FSDP, scatter_dimension=0, tiled=True
        ).astype(jnp.float32),
        lax.psum_scatter(
            partial_sums[5].astype(jnp.bfloat16), FSDP, scatter_dimension=0, tiled=True
        ).astype(jnp.float32),
        lax.psum_scatter(
            partial_sums[6].astype(jnp.bfloat16), FSDP, scatter_dimension=0, tiled=True
        ).astype(jnp.float32),
    )
    return (
        layer_out[None],
        grad_input[None],
        summed[0],
        summed[1],
        summed[2],
        summed[3],
        summed[4],
        summed[5],
        summed[6],
        grad_expert_in,
        grad_expert_out,
    )


def swap(a, flip):
    return lax.ppermute(a, FSDP, [(i, i ^ flip) for i in range(NX * NC)])


def fast_body(
    hidden,
    routes,
    attn_norm,
    ffn_norm,
    w_q,
    key_weight,
    value_weight,
    w_o,
    router,
    expert_in,
    expert_out,
    cotangent,
):
    tokens = hidden.shape[1]
    ctx = lax.axis_index(CTX)
    fsdp = lax.axis_index(FSDP)
    core = fsdp % NC
    rows = w_q.shape[0]
    quarter = expert_in.shape[1]
    kv_width = KEY_VALUE_HEADS * HEAD_SIZE
    q_width = QUERY_HEADS * HEAD_SIZE
    held = expert_in.shape[0] // NC
    bf = jnp.bfloat16
    f32 = jnp.float32
    positions = ctx * tokens + jnp.arange(tokens, dtype=jnp.int32)
    cosine_table, sine_table = (table[:, 0] for table in rope_tables(positions))
    cosine = jnp.concatenate([cosine_table] * 4, axis=1)
    sine = jnp.concatenate([-sine_table, sine_table] * 2, axis=1)
    contract_cols = (((1,), (1,)), ((), ()))
    wide = hidden[0].astype(f32)
    cot = cotangent[0]

    route = routes[0]
    indicator = (route[:, :, None] == jnp.arange(EXPERT_COUNT, dtype=jnp.int32)).astype(f32)
    part = rows // 3
    whole = (Z, Y, X, C)
    one, two, mine, *others = gather_weights(
        [w_q, key_weight, value_weight, w_o, router.T, attn_norm[None], ffn_norm[None]],
        [expert_in, expert_out],
        [
            Plan(0, (X, Z, Y, C), whole, rows=(2 * part, part)),
            Plan(1, (X, Z, Y, C), whole, rows=(part, part)),
            Plan(1, (X, Y, Z, C), whole, rows=(2 * part, part)),
            Plan(0, (Z, Y, X, C), whole, rows=(0, 2 * part)),
            Plan(1, (Z, Y, X, C), whole, rows=(0, part)),
        ],
        0,
    )
    parts = [mine, swap(mine, 2)] + [swap(other, 1) for other in others] + [swap(others[0], 3)]
    one = one.reshape(MODEL_WIDTH, -1)
    two = two.reshape(MODEL_WIDTH, -1)
    output_w = two[:, :MODEL_WIDTH]
    small = two[:, MODEL_WIDTH:]
    router_w = small[:, :EXPERT_COUNT]
    gains = lax.dot_general(
        jnp.eye(128, dtype=bf), small, contract_cols, preferred_element_type=f32
    )
    attn_gain, ffn_gain = gains[EXPERT_COUNT], gains[EXPERT_COUNT + 1]

    _, _, attention_input = rms_forward(wide, attn_gain)
    linear = jnp.dot(attention_input, one, preferred_element_type=f32)
    attention_output, log_sums, kv, cots, queries = attend(linear, cot, route, cosine, sine, 1)
    mixed = wide + jnp.dot(attention_output, output_w, preferred_element_type=f32)
    _, _, ffn_in = rms_forward(mixed, ffn_gain)
    logits = jnp.dot(ffn_in, router_w, preferred_element_type=f32)
    chosen = jnp.sum(indicator * logits[:, None, :], axis=-1)
    gates = jax.nn.softmax(chosen, axis=-1)
    gate_map = jnp.sum(indicator * gates[..., None], axis=1)
    payload = jnp.concatenate(
        [ffn_in, gate_map.astype(bf), jnp.zeros((tokens, 128 - EXPERT_COUNT), bf)], axis=1
    )
    gin, moe_part, *pieces = moe(payload, cots, parts + others[-1:], CAP, 2)
    across = [swap(pieces[j], j) for j in range(1, NX * NC)]
    gate_wide = jnp.concatenate([gate_map, jnp.zeros((tokens, 128 - EXPERT_COUNT), f32)], axis=1)
    back, layer_out, grad_mixed, grad_attn, left_small, right_small = attend_back(
        queries,
        gin,
        gate_wide,
        cot,
        ffn_gain.astype(f32)[None],
        attention_output,
        log_sums,
        kv,
        moe_part,
        two,
        mixed,
        cosine,
        sine,
        4,
    )
    *sums, grad_input = return_weights(
        [attention_input, attention_output, left_small],
        [back, grad_attn, right_small],
        one,
        hidden[0],
        attn_gain.astype(f32)[None],
        grad_mixed,
        EXPERT_COUNT,
        5,
    )
    grad_expert_in, grad_expert_out, *rest, first_gain, second_gain, layer_out, grad_input = last_outputs(
        [pieces[0]] + across,
        core,
        2 * EXPERT_HIDDEN,
        sums + [layer_out, grad_input],
        (q_width, kv_width, kv_width, MODEL_WIDTH, EXPERT_COUNT),
    )
    return (
        layer_out[None],
        grad_input[None],
        first_gain.reshape(rows),
        second_gain.reshape(rows),
        *rest[:-1],
        rest[-1].T,
        grad_expert_in.reshape(NC * held, quarter, -1),
        grad_expert_out.reshape(NC * held, quarter, -1),
    )


def fast(*args):
    return fast_body(*args)


def solution(mesh):
    placed = (
        P(FSDP, CTX, None),
        P(FSDP, CTX, None),
        P((CTX, FSDP)),
        P((CTX, FSDP)),
        P((CTX, FSDP), None),
        P((CTX, FSDP), None),
        P((CTX, FSDP), None),
        P((CTX, FSDP), None),
        P((CTX, FSDP), None),
        P(CTX, FSDP, None),
        P(CTX, FSDP, None),
        P(FSDP, CTX, None),
    )
    small = mesh.shape[CTX] == NZ * NY and mesh.shape[FSDP] == NX * NC
    return jax.shard_map(
        fast if small else local,
        mesh=mesh,
        in_specs=placed,
        out_specs=(
            P(FSDP, CTX, None),
            P(FSDP, CTX, None),
            P((CTX, FSDP)),
            P((CTX, FSDP)),
            P((CTX, FSDP), None),
            P((CTX, FSDP), None),
            P((CTX, FSDP), None),
            P((CTX, FSDP), None),
            P((CTX, FSDP), None),
            P(CTX, FSDP, None),
            P(CTX, FSDP, None),
        ),
        check_vma=False,
    )
```

profile of v0, /device:TPU:0, one launch (start us, length us, event | category | flops | bytes accessed | tf_op | source)
XLA Modules:
  0.0 448.0 jit_solution(11912833396884910985)
XLA Ops:
  0.6 0.0 copy-start
  0.7 0.0 copy-start.4
  0.7 59.9 %gather_weights.1 = (bf16[32,48,2560]{2,1,0:T(8,128)(2,1)}, bf16[32,48,1664]{2,1,0:T(8,128)(2,1)}, bf16[2,384,1536]{2,1,0:T(8,128)(2,1)}, bf16[1,384,1536]{2,1,0:T(8,128)(2,1)}, bf16[1,384,1536]{2,1,0:T(8,128)(2,1)}) custom-call(bf16[48,1536]{1,0:T(8,128)(2,1)} %refs_0_.1, bf16[48,512]{1,0:T(8,128)(2,1)} %refs_1_.1, bf16[48,512]{1,0:T(8,128)(2,1)} %refs_2_.1, ...), custom_call_target="tpu_custom_call" | custom-call | tf_op jit(solution)/shard_map/gather_weights/pallas_call | solution.py:231
  60.5 0.6 collective-permute-start.1
  61.2 0.5 collective-permute-start.3
  61.7 1.2 collective-permute-start
  62.9 0.2 collective-permute-start.2
  63.1 1.3 fusion.13
  64.3 0.6 slice_reduce_fusion
  65.0 0.0 copy-done
  65.0 0.0 copy-start.2
  65.0 0.2 fusion.5
  65.1 0.0 copy-start.5
  65.2 0.0 copy-done.4
  65.2 0.7 copy.29
  65.9 0.3 fusion.17
  66.2 0.8 pad_maximum_fusion
  67.0 5.6 %fusion.9.linear = f32[128,2560]{1,0:T(8,128)} fusion(bf16[1536,2560]{1,0:T(8,128)(2,1)} %bitcast.26, bf16[1,128,1536]{2,1,0:T(8,128)(2,1)S(1)} %copy-done, f32[1536]{0:T(1024)S(1)} %get-tuple-element.86, f32[128]{0:T(128)S(1)} %add_rsqrt_fusion.1), kind=kOutput, calls=%fused_computation.12 | convolution fusion | flops 1007419392 | bytes 9574912 | tf_op jit(solution)/shard_map/dot_general | solution.py:1775
  72.6 0.0 copy-done.2
  72.6 0.0 copy-done.5
  72.6 76.2 %attend.1 = (bf16[128,1536]{1,0:T(8,128)(2,1)}, f32[384,128]{1,0:T(8,128)}, bf16[8,128,1024]{2,1,0:T(8,128)(2,1)}, bf16[16,128,1664]{2,1,0:T(8,128)(2,1)}, bf16[8,384,128]{2,1,0:T(8,128)(2,1)}) custom-call(f32[128,2560]{1,0:T(8,128)} %fusion.9.linear, f32[128,1536]{1,0:T(8,128)} %bitcast.33, s32[128,8]{1,0:T(8,128)} %bitcast.35, ...), custom_call_target="tpu_custom_call" | custom-call | tf_op jit(solution)/shard_map/attend/pallas_call | solution.py:1040
  148.8 3.3 multiply_reduce_fusion
  152.1 0.0 copy-start.1
  152.2 0.9 copy-done.1
  153.0 0.1 multiply_convert_fusion
  153.2 1.3 fusion.11
  154.5 0.0 copy-start.3
  154.6 0.6 copy-done.3
  155.2 0.1 copy.32
  155.3 0.9 concatenate.14.refs_0_
  156.1 0.0 collective-permute-done.1.refs_4_
  156.2 0.0 collective-permute-done.2.refs_5_
  156.2 0.0 collective-permute-done.3.refs_6_
  156.2 0.0 collective-permute-done.refs_3_
  156.2 109.2 %experts.1 = (f32[128,1664]{1,0:T(8,128)}, bf16[16,128,1536]{2,1,0:T(8,128)(2,1)}, bf16[2,384,1536]{2,1,0:T(8,128)(2,1)}, bf16[2,384,1536]{2,1,0:T(8,128)(2,1)},...) custom-call(bf16[128,1664]{1,0:T(8,128)(2,1)} %concatenate.14.refs_0_, ...), custom_call_target="tpu_custom_call" | custom-call | tf_op jit(solution)/shard_map/experts/pallas_call | solution.py:743
  265.4 0.1 collective-permute-start.4
  265.5 2.4 collective-permute-start.5
  267.9 0.0 collective-permute-start.6
  267.9 0.8 copy.33
  268.7 0.6 concatenate.15.refs_2_
  269.4 1.9 fusion.7.refs_0_
  271.3 81.1 %attend_back.1 = (bf16[128,2560]{1,0:T(8,128)(2,1)}, bf16[128,1536]{1,0:T(8,128)(2,1)}, f32[128,1536]{1,0:T(8,128)}, bf16[128,1536]{1,0:T(8,128)(2,1)}, bf16[384...) custom-call(bf16[8,384,128]{2,1,0:T(8,128)(2,1)} %get-tuple-element.59.refs_0_, f32[128,1664]{1,0:T(8,128)} %get-tuple-element.60.refs_1_, ...), custom_call_target="tpu_custom_call" | custom-call | tf_op jit(solution)/shard_map/attend_back/pallas_call | solution.py:1220
  352.4 85.9 %return_weights.1 = (f32[48,2560]{1,0:T(8,128)}, f32[48,1536]{1,0:T(8,128)}, f32[48,128]{1,0:T(8,128)}, f32[128,1536]{1,0:T(8,128)}) custom-call(bf16[128,1536]{1,0:T(8,128)(2,1)} %fusion.7.refs_0_, bf16[128,2560]{1,0:T(8,128)(2,1)} %get-tuple-element.64.refs_1_, bf16[128,1536]{1,0:T(8,128)(2,1)} %get-tuple-element.50.refs_5_.refs_2_, ...), custom_call_target="tpu_custom_call" | custom-call | tf_op jit(solution)/shard_map/return_weights/pallas_call | solution.py:877
  438.3 0.0 collective-permute-done.4.core_part
  438.3 0.0 collective-permute-done.5.x_part
  438.3 0.0 collective-permute-done.6.both_part
  438.4 9.2 %last_outputs.1 = (f32[2,2,384,1024]{3,2,1,0:T(8,128)}, f32[2,2,384,512]{3,2,1,0:T(8,128)}, f32[48,1536]{1,0:T(8,128)}, f32[48,512]{1,0:T(8,128)}, f32[48,512]{1...) custom-call(s32[1]{0:T(128)} %bitcast.core_ref, ...), custom_call_target="tpu_custom_call" | custom-call | tf_op jit(solution)/shard_map/last_outputs/pallas_call | solution.py:1287
  (11 shorter events, 0.1 us)
Async XLA Ops:
  0.6 64.3 %copy-start = (bf16[1,128,1536]{2,1,0:T(8,128)(2,1)S(1)}, bf16[1,128,1536]{2,1,0:T(8,128)(2,1)}, u32[]{:S(2)}) copy-start(bf16[1,128,1536]{2,1,0:T(8,128)(2,1)} %param.12) | copy-start | bytes 1179652
  0.7 64.5 %copy-start.4 = (s32[1,128,8]{1,2,0:T(8,128)S(1)}, s32[1,128,8]{1,2,0:T(8,128)}, u32[]{:S(2)}) copy-start(s32[1,128,8]{1,2,0:T(8,128)} %param.13) | copy-start | bytes 12292
  60.5 95.6 %collective-permute-start.1 = (bf16[1,384,1536]{2,1,0:T(8,128)(2,1)}, bf16[1,384,1536]{2,1,0:T(8,128)(2,1)}, u32[]{:S(2)}, u32[]{:S(2)}) collective-permute-start(bf16[1,384,1536]{2,1,0:T(8,128)(2,1)} %get-tuple-element.53), channel_id=1, source_target_pairs={{0,1},{1,0},{2,3},{3,2},{4,5},{5,4},{6,7},{7,6},{8,9},{9,8},{10,11... | collective-permute-start | bytes 3538952 | tf_op jit(solution)/shard_map/ppermute | solution.py:1711
  61.2 95.0 %collective-permute-start.3 = (bf16[1,384,1536]{2,1,0:T(8,128)(2,1)}, bf16[1,384,1536]{2,1,0:T(8,128)(2,1)}, u32[]{:S(2)}, u32[]{:S(2)}) collective-permute-start(bf16[1,384,1536]{2,1,0:T(8,128)(2,1)} %get-tuple-element.53), channel_id=1, source_target_pairs={{0,3},{1,2},{2,1},{3,0},{4,7},{5,6},{6,5},{7,4},{8,11},{9,10},{10,... | collective-permute-start | bytes 3538952 | tf_op jit(solution)/shard_map/ppermute | solution.py:1711
  61.7 94.5 %collective-permute-start = (bf16[2,384,1536]{2,1,0:T(8,128)(2,1)}, bf16[2,384,1536]{2,1,0:T(8,128)(2,1)}, u32[]{:S(2)}, u32[]{:S(2)}) collective-permute-start(bf16[2,384,1536]{2,1,0:T(8,128)(2,1)} %get-tuple-element.52.refs_2_), channel_id=1, source_target_pairs={{0,2},{1,3},{2,0},{3,1},{4,6},{5,7},{6,4},{7,5},{8,10},{9,11},{10,... | collective-permute-start | bytes 7077896 | tf_op jit(solution)/shard_map/ppermute | solution.py:1711
  62.9 93.2 %collective-permute-start.2 = (bf16[1,384,1536]{2,1,0:T(8,128)(2,1)}, bf16[1,384,1536]{2,1,0:T(8,128)(2,1)}, u32[]{:S(2)}, u32[]{:S(2)}) collective-permute-start(bf16[1,384,1536]{2,1,0:T(8,128)(2,1)} %get-tuple-element.54.refs_7_), channel_id=1, source_target_pairs={{0,1},{1,0},{2,3},{3,2},{4,5},{5,4},{6,7},{7,6},{8,9},{9,8},{10,11... | collective-permute-start | bytes 3538952 | tf_op jit(solution)/shard_map/ppermute | solution.py:1711
  65.0 7.7 %copy-start.2 = (f32[1536]{0:T(1024)}, f32[1536]{0:T(1024)S(1)}, u32[]{:S(2)}) copy-start(f32[1536]{0:T(1024)S(1)} %get-tuple-element.86) | copy-start | bytes 18436
  65.1 7.5 %copy-start.5 = (f32[128]{0:T(128)}, f32[128]{0:T(128)S(1)}, u32[]{:S(2)}) copy-start(f32[128]{0:T(128)S(1)} %add_rsqrt_fusion.1) | copy-start | bytes 1540
  152.1 0.9 copy-start.1
  154.5 0.6 copy-start.3
  265.4 172.9 %collective-permute-start.4 = (bf16[2,384,1536]{2,1,0:T(8,128)(2,1)}, bf16[2,384,1536]{2,1,0:T(8,128)(2,1)}, u32[]{:S(2)}, u32[]{:S(2)}) collective-permute-start(bf16[2,384,1536]{2,1,0:T(8,128)(2,1)} %get-tuple-element.56), channel_id=1, source_target_pairs={{0,1},{1,0},{2,3},{3,2},{4,5},{5,4},{6,7},{7,6},{8,9},{9,8},{10,11... | collective-permute-start | bytes 7077896 | tf_op jit(solution)/shard_map/ppermute | solution.py:1711
  265.5 172.9 %collective-permute-start.5 = (bf16[2,384,1536]{2,1,0:T(8,128)(2,1)}, bf16[2,384,1536]{2,1,0:T(8,128)(2,1)}, u32[]{:S(2)}, u32[]{:S(2)}) collective-permute-start(bf16[2,384,1536]{2,1,0:T(8,128)(2,1)} %get-tuple-element.57), channel_id=1, source_target_pairs={{0,2},{1,3},{2,0},{3,1},{4,6},{5,7},{6,4},{7,5},{8,10},{9,11},{10,... | collective-permute-start | bytes 7077896 | tf_op jit(solution)/shard_map/ppermute | solution.py:1711
  267.9 170.5 %collective-permute-start.6 = (bf16[2,384,1536]{2,1,0:T(8,128)(2,1)}, bf16[2,384,1536]{2,1,0:T(8,128)(2,1)}, u32[]{:S(2)}, u32[]{:S(2)}) collective-permute-start(bf16[2,384,1536]{2,1,0:T(8,128)(2,1)} %get-tuple-element.58), channel_id=1, source_target_pairs={{0,3},{1,2},{2,1},{3,0},{4,7},{5,6},{6,5},{7,4},{8,11},{9,10},{10,... | collective-permute-start | bytes 7077896 | tf_op jit(solution)/shard_map/ppermute | solution.py:1711
where the time goes:
time: 454 us; the launch traced here: 448 us
  Pallas kernels  421 us (93%)
  matrix products  11.4 us (3%)
  local copies, waits for them, and re-layouts  5.26 us (1%)
  starting transfers between devices  5.01 us (1%)
    pallas_call x1, Pallas kernels, moe(): pl.pallas_call(functools.partial(moe_kernel, plans, back, width, hidden,...  109 us
    pallas_call x1, Pallas kernels, return_weights(): pl.pallas_call(functools.partial(weights_kernel, plans, gain_at), out_sha...  85.9 us
    pallas_call x1, Pallas kernels, attend_back(): pl.pallas_call(functools.partial(attend_back_kernel, plans), out_shape=[j...  81.1 us
    pallas_call x1, Pallas kernels, attend(): pl.pallas_call(functools.partial(attend_kernel, plans), out_shape=[jax.Sh...  76.2 us
    pallas_call x1, Pallas kernels, gather_weights(): pl.pallas_call(functools.partial(gather_kernel, plans), out_shape=[jax.Sh...  59.9 us
    pallas_call x1, Pallas kernels, last_outputs(): pl.pallas_call(last_kernel, grid_spec=pltpu.PrefetchScalarGridSpec(num_sc...  9.17 us
  transfers between devices with their start and end apart: 7, of which 0 were waited for; matrix products, arithmetic and copies ran while one was open for 4% of the time, Pallas kernels for 54%

commit v1 on v0

--- a/solution.py
+++ b/solution.py
@@ -815,10 +815,11 @@
                 group, rows // group, cn
             )
 
-    def round_of(some, t):
+    def late(some, t):
         for way in some:
             for step in way.at_time(t):
-                step()
+                if not (isinstance(step, functools.partial) and len(step.args) == 2 and step.args[0] == 0):
+                    step()
 
     for t in range(NZ):
         for n, way in enumerate(ways):
@@ -828,7 +829,10 @@
                 meet(count_here)
             way.first(far[t])
         if t > 0:
-            round_of(ways, t - 1)
+            for way in ways:
+                way.level(0, far[t - 1])
+    for way in ways:
+        way.level(0, far[-1])
     fetch.wait()
     for c0, cn in columns_of(grad_in.shape[1]):
         grad_in[:, c0 : c0 + cn] = lax.dot_general(
@@ -849,11 +853,15 @@
     for k in far:
         products([(left_small, right_small), (halves, column)], held[-1], k)
         small_way.first(k)
-    late = [(0, 1, 2), (3, 4), (5,), (6,)]
-    for n, t in enumerate(range(NZ - 1, NZ + 3)):
-        round_of(ways, t)
-        for t_small in late[n]:
-            round_of([small_way], t_small)
+    for k in far:
+        small_way.level(0, k)
+    y_first, x_first, small = ways[:2], ways[2:], [small_way]
+    for some, t in (
+        (y_first, 1), (y_first, 2), (x_first, 1), (x_first, 2), (y_first, 3), (x_first, 3), (small, 1), (x_first, 4),
+        (y_first, 4), (small, 2), (small, 3), (y_first, 5), (x_first, 5), (small, 4), (y_first, 6), (x_first, 6),
+        (small, 5), (small, 6),
+    ):
+        late(some, t)
     for n, way in enumerate(ways):
         width = held[n].shape[2]
         way.last(outs[n // 2].at[:, pl.ds(n % 2 * width, width)])

time: 454 us -> 467 us (1.029)
  Pallas kernels: 421 us -> 434 us
    pallas_call x1, Pallas kernels: 85.9 us -> 98.7 us  [return_weights(): pl.pallas_call(functools.partial(weights_kernel, plans, gain_at), out_sha...]
  transfers between devices with their start and end apart: 7 -> 7, of which waited for: 0 -> 0; matrix products, arithmetic and copies ran while one was open for 4% -> 4% of each run, Pallas kernels for 54% -> 56%
where the time goes in v1:
time: 467 us; the launch traced here: 461 us
  Pallas kernels  434 us (93%)
  matrix products  11.4 us (2%)
  local copies, waits for them, and re-layouts  5.26 us (1%)
  starting transfers between devices  5.01 us (1%)
    pallas_call x1, Pallas kernels, moe(): pl.pallas_call(functools.partial(moe_kernel, plans, back, width, hidden,...  109 us
    pallas_call x1, Pallas kernels, return_weights(): pl.pallas_call(functools.partial(weights_kernel, plans, gain_at), out_sha...  98.7 us
    pallas_call x1, Pallas kernels, attend_back(): pl.pallas_call(functools.partial(attend_back_kernel, plans), out_shape=[j...  81.1 us
    pallas_call x1, Pallas kernels, attend(): pl.pallas_call(functools.partial(attend_kernel, plans), out_shape=[jax.Sh...  76.2 us
    pallas_call x1, Pallas kernels, gather_weights(): pl.pallas_call(functools.partial(gather_kernel, plans), out_shape=[jax.Sh...  59.9 us
  transfers between devices with their start and end apart: 7, of which 0 were waited for; matrix products, arithmetic and copies ran while one was open for 4% of the time, Pallas kernels for 56%

profile of v1, /device:TPU:0, one launch (start us, length us, event | category | flops | bytes accessed | tf_op | source)
XLA Modules:
  0.0 460.8 jit_solution(318926222944893563)
XLA Ops:
  0.6 0.0 copy-start
  0.7 0.0 copy-start.4
  0.7 59.9 %gather_weights.1 = (bf16[32,48,2560]{2,1,0:T(8,128)(2,1)}, bf16[32,48,1664]{2,1,0:T(8,128)(2,1)}, bf16[2,384,1536]{2,1,0:T(8,128)(2,1)}, bf16[1,384,1536]{2,1,0:T(8,128)(2,1)}, bf16[1,384,1536]{2,1,0:T(8,128)(2,1)}) custom-call(bf16[48,1536]{1,0:T(8,128)(2,1)} %refs_0_.1, bf16[48,512]{1,0:T(8,128)(2,1)} %refs_1_.1, bf16[48,512]{1,0:T(8,128)(2,1)} %refs_2_.1, ...), custom_call_target="tpu_custom_call" | custom-call | tf_op jit(solution)/shard_map/gather_weights/pallas_call | solution.py:231
  60.5 0.6 collective-permute-start.1
  61.2 0.5 collective-permute-start.3
  61.7 1.2 collective-permute-start
  62.9 0.2 collective-permute-start.2
  63.1 1.3 fusion.13
  64.3 0.6 slice_reduce_fusion
  65.0 0.0 copy-done
  65.0 0.0 copy-start.2
  65.0 0.2 fusion.5
  65.1 0.0 copy-start.5
  65.2 0.0 copy-done.4
  65.2 0.7 copy.29
  65.9 0.3 fusion.17
  66.2 0.8 pad_maximum_fusion
  67.0 5.6 %fusion.9.linear = f32[128,2560]{1,0:T(8,128)} fusion(bf16[1536,2560]{1,0:T(8,128)(2,1)} %bitcast.26, bf16[1,128,1536]{2,1,0:T(8,128)(2,1)S(1)} %copy-done, f32[1536]{0:T(1024)S(1)} %get-tuple-element.86, f32[128]{0:T(128)S(1)} %add_rsqrt_fusion.1), kind=kOutput, calls=%fused_computation.12 | convolution fusion | flops 1007419392 | bytes 9574912 | tf_op jit(solution)/shard_map/dot_general | solution.py:1783
  72.6 0.0 copy-done.2
  72.6 0.0 copy-done.5
  72.6 76.2 %attend.1 = (bf16[128,1536]{1,0:T(8,128)(2,1)}, f32[384,128]{1,0:T(8,128)}, bf16[8,128,1024]{2,1,0:T(8,128)(2,1)}, bf16[16,128,1664]{2,1,0:T(8,128)(2,1)}, bf16[8,384,128]{2,1,0:T(8,128)(2,1)}) custom-call(f32[128,2560]{1,0:T(8,128)} %fusion.9.linear, f32[128,1536]{1,0:T(8,128)} %bitcast.33, s32[128,8]{1,0:T(8,128)} %bitcast.35, ...), custom_call_target="tpu_custom_call" | custom-call | tf_op jit(solution)/shard_map/attend/pallas_call | solution.py:1048
  148.8 3.3 multiply_reduce_fusion
  152.1 0.0 copy-start.1
  152.2 0.9 copy-done.1
  153.0 0.1 multiply_convert_fusion
  153.2 1.3 fusion.11
  154.5 0.0 copy-start.3
  154.6 0.6 copy-done.3
  155.2 0.1 copy.32
  155.3 0.9 concatenate.14.refs_0_
  156.1 0.0 collective-permute-done.1.refs_4_
  156.2 0.0 collective-permute-done.2.refs_5_
  156.2 0.0 collective-permute-done.3.refs_6_
  156.2 0.0 collective-permute-done.refs_3_
  156.2 109.2 %experts.1 = (f32[128,1664]{1,0:T(8,128)}, bf16[16,128,1536]{2,1,0:T(8,128)(2,1)}, bf16[2,384,1536]{2,1,0:T(8,128)(2,1)}, bf16[2,384,1536]{2,1,0:T(8,128)(2,1)},...) custom-call(bf16[128,1664]{1,0:T(8,128)(2,1)} %concatenate.14.refs_0_, ...), custom_call_target="tpu_custom_call" | custom-call | tf_op jit(solution)/shard_map/experts/pallas_call | solution.py:743
  265.4 0.1 collective-permute-start.4
  265.5 2.4 collective-permute-start.5
  267.9 0.0 collective-permute-start.6
  267.9 0.8 copy.33
  268.7 0.6 concatenate.15.refs_2_
  269.4 1.9 fusion.7.refs_0_
  271.3 81.1 %attend_back.1 = (bf16[128,2560]{1,0:T(8,128)(2,1)}, bf16[128,1536]{1,0:T(8,128)(2,1)}, f32[128,1536]{1,0:T(8,128)}, bf16[128,1536]{1,0:T(8,128)(2,1)}, bf16[384...) custom-call(bf16[8,384,128]{2,1,0:T(8,128)(2,1)} %get-tuple-element.59.refs_0_, f32[128,1664]{1,0:T(8,128)} %get-tuple-element.60.refs_1_, ...), custom_call_target="tpu_custom_call" | custom-call | tf_op jit(solution)/shard_map/attend_back/pallas_call | solution.py:1228
  352.4 98.7 %return_weights.1 = (f32[48,2560]{1,0:T(8,128)}, f32[48,1536]{1,0:T(8,128)}, f32[48,128]{1,0:T(8,128)}, f32[128,1536]{1,0:T(8,128)}) custom-call(bf16[128,1536]{1,0:T(8,128)(2,1)} %fusion.7.refs_0_, bf16[128,2560]{1,0:T(8,128)(2,1)} %get-tuple-element.64.refs_1_, bf16[128,1536]{1,0:T(8,128)(2,1)} %get-tuple-element.50.refs_5_.refs_2_, ...), custom_call_target="tpu_custom_call" | custom-call | tf_op jit(solution)/shard_map/return_weights/pallas_call | solution.py:885
  451.2 0.0 collective-permute-done.4.core_part
  451.2 0.0 collective-permute-done.5.x_part
  451.2 0.0 collective-permute-done.6.both_part
  451.2 9.2 %last_outputs.1 = (f32[2,2,384,1024]{3,2,1,0:T(8,128)}, f32[2,2,384,512]{3,2,1,0:T(8,128)}, f32[48,1536]{1,0:T(8,128)}, f32[48,512]{1,0:T(8,128)}, f32[48,512]{1...) custom-call(s32[1]{0:T(128)} %bitcast.core_ref, ...), custom_call_target="tpu_custom_call" | custom-call | tf_op jit(solution)/shard_map/last_outputs/pallas_call | solution.py:1295
  (11 shorter events, 0.1 us)
Async XLA Ops:
  0.6 64.3 %copy-start = (bf16[1,128,1536]{2,1,0:T(8,128)(2,1)S(1)}, bf16[1,128,1536]{2,1,0:T(8,128)(2,1)}, u32[]{:S(2)}) copy-start(bf16[1,128,1536]{2,1,0:T(8,128)(2,1)} %param.12) | copy-start | bytes 1179652
  0.7 64.5 %copy-start.4 = (s32[1,128,8]{1,2,0:T(8,128)S(1)}, s32[1,128,8]{1,2,0:T(8,128)}, u32[]{:S(2)}) copy-start(s32[1,128,8]{1,2,0:T(8,128)} %param.13) | copy-start | bytes 12292
  60.5 95.6 %collective-permute-start.1 = (bf16[1,384,1536]{2,1,0:T(8,128)(2,1)}, bf16[1,384,1536]{2,1,0:T(8,128)(2,1)}, u32[]{:S(2)}, u32[]{:S(2)}) collective-permute-start(bf16[1,384,1536]{2,1,0:T(8,128)(2,1)} %get-tuple-element.53), channel_id=1, source_target_pairs={{0,1},{1,0},{2,3},{3,2},{4,5},{5,4},{6,7},{7,6},{8,9},{9,8},{10,11... | collective-permute-start | bytes 3538952 | tf_op jit(solution)/shard_map/ppermute | solution.py:1719
  61.2 95.0 %collective-permute-start.3 = (bf16[1,384,1536]{2,1,0:T(8,128)(2,1)}, bf16[1,384,1536]{2,1,0:T(8,128)(2,1)}, u32[]{:S(2)}, u32[]{:S(2)}) collective-permute-start(bf16[1,384,1536]{2,1,0:T(8,128)(2,1)} %get-tuple-element.53), channel_id=1, source_target_pairs={{0,3},{1,2},{2,1},{3,0},{4,7},{5,6},{6,5},{7,4},{8,11},{9,10},{10,... | collective-permute-start | bytes 3538952 | tf_op jit(solution)/shard_map/ppermute | solution.py:1719
  61.7 94.5 %collective-permute-start = (bf16[2,384,1536]{2,1,0:T(8,128)(2,1)}, bf16[2,384,1536]{2,1,0:T(8,128)(2,1)}, u32[]{:S(2)}, u32[]{:S(2)}) collective-permute-start(bf16[2,384,1536]{2,1,0:T(8,128)(2,1)} %get-tuple-element.52.refs_2_), channel_id=1, source_target_pairs={{0,2},{1,3},{2,0},{3,1},{4,6},{5,7},{6,4},{7,5},{8,10},{9,11},{10,... | collective-permute-start | bytes 7077896 | tf_op jit(solution)/shard_map/ppermute | solution.py:1719
  62.9 93.2 %collective-permute-start.2 = (bf16[1,384,1536]{2,1,0:T(8,128)(2,1)}, bf16[1,384,1536]{2,1,0:T(8,128)(2,1)}, u32[]{:S(2)}, u32[]{:S(2)}) collective-permute-start(bf16[1,384,1536]{2,1,0:T(8,128)(2,1)} %get-tuple-element.54.refs_7_), channel_id=1, source_target_pairs={{0,1},{1,0},{2,3},{3,2},{4,5},{5,4},{6,7},{7,6},{8,9},{9,8},{10,11... | collective-permute-start | bytes 3538952 | tf_op jit(solution)/shard_map/ppermute | solution.py:1719
  65.0 7.7 %copy-start.2 = (f32[1536]{0:T(1024)}, f32[1536]{0:T(1024)S(1)}, u32[]{:S(2)}) copy-start(f32[1536]{0:T(1024)S(1)} %get-tuple-element.86) | copy-start | bytes 18436
  65.1 7.5 %copy-start.5 = (f32[128]{0:T(128)}, f32[128]{0:T(128)S(1)}, u32[]{:S(2)}) copy-start(f32[128]{0:T(128)S(1)} %add_rsqrt_fusion.1) | copy-start | bytes 1540
  152.1 0.9 copy-start.1
  154.5 0.6 copy-start.3
  265.4 185.8 %collective-permute-start.4 = (bf16[2,384,1536]{2,1,0:T(8,128)(2,1)}, bf16[2,384,1536]{2,1,0:T(8,128)(2,1)}, u32[]{:S(2)}, u32[]{:S(2)}) collective-permute-start(bf16[2,384,1536]{2,1,0:T(8,128)(2,1)} %get-tuple-element.56), channel_id=1, source_target_pairs={{0,1},{1,0},{2,3},{3,2},{4,5},{5,4},{6,7},{7,6},{8,9},{9,8},{10,11... | collective-permute-start | bytes 7077896 | tf_op jit(solution)/shard_map/ppermute | solution.py:1719
  265.5 185.7 %collective-permute-start.5 = (bf16[2,384,1536]{2,1,0:T(8,128)(2,1)}, bf16[2,384,1536]{2,1,0:T(8,128)(2,1)}, u32[]{:S(2)}, u32[]{:S(2)}) collective-permute-start(bf16[2,384,1536]{2,1,0:T(8,128)(2,1)} %get-tuple-element.57), channel_id=1, source_target_pairs={{0,2},{1,3},{2,0},{3,1},{4,6},{5,7},{6,4},{7,5},{8,10},{9,11},{10,... | collective-permute-start | bytes 7077896 | tf_op jit(solution)/shard_map/ppermute | solution.py:1719
  267.9 183.3 %collective-permute-start.6 = (bf16[2,384,1536]{2,1,0:T(8,128)(2,1)}, bf16[2,384,1536]{2,1,0:T(8,128)(2,1)}, u32[]{:S(2)}, u32[]{:S(2)}) collective-permute-start(bf16[2,384,1536]{2,1,0:T(8,128)(2,1)} %get-tuple-element.58), channel_id=1, source_target_pairs={{0,3},{1,2},{2,1},{3,0},{4,7},{5,6},{6,5},{7,4},{8,11},{9,10},{10,... | collective-permute-start | bytes 7077896 | tf_op jit(solution)/shard_map/ppermute | solution.py:1719
